TPU v7x, 32 devices: a whole 2x2x4 slice. The times are simulated.
32 devices in a mesh: grp: 4 (over z), slab: 8 (over y, x, core).
Axes of the slice: x: 2, y: 2, z: 4, core: 2. Of those that a mesh axis runs over, the one named last changes fastest.
Arguments:
- tensor: float32 [672, 64, 672], P('grp', 'slab'), may hold values from -20 to 20
- start_one: float32 [672, 96], replicated, may hold values from -6 to 6
- start_two: float32 [672, 96], replicated, may hold values from -6 to 6
Outputs:
- basis_one: float32 [672, 96], replicated
- basis_two: float32 [672, 96], replicated
- core: float32 [96, 64, 96], P('grp', 'slab')
All inputs are finite; a program needn't handle non-finite values.
Results may differ from a plain program's by a relative error of at most 0.0003.
Values sent between devices are 32-bit elements; how exact they have to be, the bound alone decides.
No kernel may reach another device: no remote copies, remote signals or barrier semaphores. Data moves between devices by JAX's collectives and lax.ppermute only.
A program may use at most 64 MiB of HBM per device.

v0:
```python
import jax
import jax.numpy as jnp
from jax import lax
from jax.sharding import PartitionSpec as P

ITERS = 2


HIGH = lax.Precision.HIGHEST


def orthonormal(widened):
    cross = jnp.dot(widened.T, widened, precision=HIGH)
    lower_small = jnp.linalg.cholesky(cross)
    return lax.linalg.triangular_solve(
        lower_small, widened, left_side=False, lower=True, transpose_a=True
    )


def iterate_basis(gram, start):
    current = start
    for _ in range(ITERS):
        current = orthonormal(jnp.dot(gram, current, precision=HIGH))
    return current


def local(tensor, start_one, start_two):
    block_gram = jnp.einsum("jmi,jmk->ik", tensor, tensor, precision=HIGH)
    gram_one = lax.psum(block_gram, ("grp", "slab"))
    basis_one = iterate_basis(gram_one, start_one)
    reduced = jnp.einsum("jmi,ia->jma", tensor, basis_one, precision=HIGH)
    regrouped = lax.all_to_all(reduced, "grp", split_axis=1, concat_axis=0, tiled=True)
    block_second = jnp.einsum("jma,kma->jk", regrouped, regrouped, precision=HIGH)
    gram_two = lax.psum(block_second, ("grp", "slab"))
    basis_two = iterate_basis(gram_two, start_two)
    core_block = jnp.einsum("jb,jma->bma", basis_two, regrouped, precision=HIGH)
    core = lax.all_to_all(core_block, "grp", split_axis=0, concat_axis=1, tiled=True)
    return (basis_one, basis_two, core)


def solution(mesh):
    in_specs = (P("grp", "slab", None), P(), P())
    out_specs = (P(), P(), P("grp", "slab", None))
    return jax.shard_map(local, mesh=mesh, in_specs=in_specs, out_specs=out_specs, check_vma=False)
```

profile of v0, /device:TPU:0, one launch (start us, length us, event | category | flops | bytes accessed | tf_op | source)
XLA Modules:
  0.0 428.3 jit_solution(15188821805483427743)
XLA Ops:
  7.2 18.1 %fusion.4 = f32[672,672]{1,0:T(8,128)} fusion(f32[168,8,672]{2,1,0:T(8,128)} %param.6), kind=kOutput, calls=%fused_computation.5 | convolution fusion | flops 7283146752 | bytes 5419008 | tf_op jit(solution)/shard_map/jmi,jmk->ik/dot_general | solution.py:28
  25.6 136.9 %all-reduce.3.cloned.1.call-done = f32[672,672]{1,0:T(8,128)} async-done(((f32[672,672]{1,0:T(8,128)}), f32[672,672]{1,0:T(8,128)}) %all-reduce.3.cloned.1.call-update) | async-done | bytes 1806352 | tf_op jit(solution)/shard_map/psum | solution.py:29
  162.5 3.7 fusion.29
  166.7 8.8 %cholesky.74 = f32[96,96]{1,0:T(8,128)S(1)} custom-call(f32[96,96]{1,0:T(8,128)S(1)} %fusion.26), custom_call_target="Cholesky" | custom-call | tf_op jit(solution)/shard_map/jit(cholesky)/cholesky | solution.py:14
  176.1 0.7 fusion.13
  176.8 7.4 %custom-call.8 = f32[1,96,96]{1,2,0:T(8,128)S(1)} custom-call(f32[1,96,96]{2,1,0:T(8,128)S(1)} %fusion.13), custom_call_target="InvertDiagBlocksLowerTriangular" | custom-call | tf_op jit(solution)/shard_map/triangular_solve/custom-call.0 | solution.py:15
  184.6 2.0 fusion.31
  187.1 8.8 %cholesky.85 = f32[96,96]{1,0:T(8,128)S(1)} custom-call(f32[96,96]{1,0:T(8,128)S(1)} %fusion.24), custom_call_target="Cholesky" | custom-call | tf_op jit(solution)/shard_map/jit(cholesky)/cholesky | solution.py:14
  196.5 0.7 fusion.14
  197.2 7.4 %custom-call.9 = f32[1,96,96]{1,2,0:T(8,128)S(1)} custom-call(f32[1,96,96]{2,1,0:T(8,128)S(1)} %fusion.14), custom_call_target="InvertDiagBlocksLowerTriangular" | custom-call | tf_op jit(solution)/shard_map/triangular_solve/custom-call.0 | solution.py:15
  205.0 6.5 %fusion.7 = f32[168,8,96]{2,0,1:T(8,128)S(1)} fusion(f32[168,8,672]{2,1,0:T(8,128)} %param.6, f32[96,672]{1,0:T(8,128)S(1)} %fusion.22), kind=kOutput, calls=%fused_computation.6 | convolution fusion | flops 1040449536 | bytes 4386816 | tf_op jit(solution)/shard_map/jmi,ia->jma/dot_general | solution.py:31
  211.5 19.8 %all_to_all.36 = f32[168,8,96]{2,0,1:T(8,128)S(1)} all-to-all(f32[168,8,96]{2,0,1:T(8,128)S(1)} %fusion.7), channel_id=1, replica_groups=mesh['grp'=4,'slab'=8] {'grp'}, dimensions={1} | all-to-all | bytes 1032192 | tf_op jit(solution)/shard_map/all_to_all | solution.py:32
  231.4 3.1 convolution_bitcast_fusion
  234.5 133.3 %all-reduce.5.cloned.1.call-done = f32[672,672]{1,0:T(8,128)} async-done(((f32[672,672]{1,0:T(8,128)}), f32[672,672]{1,0:T(8,128)}) %all-reduce.5.cloned.1.call-update) | async-done | bytes 1806352 | tf_op jit(solution)/shard_map/psum | solution.py:34
  367.7 3.7 fusion.33
  371.9 8.8 %cholesky.96 = f32[96,96]{1,0:T(8,128)S(1)} custom-call(f32[96,96]{1,0:T(8,128)S(1)} %fusion.21), custom_call_target="Cholesky" | custom-call | tf_op jit(solution)/shard_map/jit(cholesky)/cholesky | solution.py:14
  381.4 0.7 fusion.15
  382.0 7.4 %custom-call.10 = f32[1,96,96]{1,2,0:T(8,128)S(1)} custom-call(f32[1,96,96]{2,1,0:T(8,128)S(1)} %fusion.15), custom_call_target="InvertDiagBlocksLowerTriangular" | custom-call | tf_op jit(solution)/shard_map/triangular_solve/custom-call.0 | solution.py:15
  389.9 2.0 fusion.35
  392.3 9.0 %cholesky.107 = f32[96,96]{1,0:T(8,128)S(1)} custom-call(f32[96,96]{1,0:T(8,128)S(1)} %fusion.19), custom_call_target="Cholesky" | custom-call | tf_op jit(solution)/shard_map/jit(cholesky)/cholesky | solution.py:14
  402.0 0.7 fusion.16
  402.7 7.4 %custom-call.11 = f32[1,96,96]{1,2,0:T(8,128)S(1)} custom-call(f32[1,96,96]{2,1,0:T(8,128)S(1)} %fusion.16), custom_call_target="InvertDiagBlocksLowerTriangular" | custom-call | tf_op jit(solution)/shard_map/triangular_solve/custom-call.0 | solution.py:15
  411.1 9.2 %all_to_all.37 = f32[96,2,96]{2,1,0:T(2,128)S(1)} all-to-all(f32[96,2,96]{2,1,0:T(2,128)S(1)} %copy.38), channel_id=1, replica_groups=mesh['grp'=4,'slab'=8] {'grp'}, dimensions={0} | all-to-all | bytes 147456 | tf_op jit(solution)/shard_map/all_to_all | solution.py:37
  420.3 0.7 copy.39
  (41 shorter events, 7.3 us)
Async XLA Ops:
  7.2 155.3 %copy-start = (f32[672,96]{0,1:T(8,128)S(1)}, f32[672,96]{0,1:T(8,128)}, u32[]{:S(2)}) copy-start(f32[672,96]{0,1:T(8,128)} %param.7) | copy-start | bytes 774148
  7.2 155.3 %all-reduce.3.cloned.1.call-start = ((), (), s32[]{:S(2)}) async-start(), calls=%async_computation.2 | async-start | bytes 4128768 | tf_op jit(solution)/shard_map/psum | solution.py:29
  25.3 342.4 %all-reduce.5.cloned.1.call-start = ((), (), s32[]{:S(2)}) async-start(), calls=%async_computation.3 | async-start | bytes 4128768 | tf_op jit(solution)/shard_map/psum | solution.py:34
  162.5 22.1 %copy-start.1 = (f32[672,672]{1,0:T(8,128)S(1)}, f32[672,672]{1,0:T(8,128)}, u32[]{:S(2)}) copy-start(f32[672,672]{1,0:T(8,128)} %all-reduce.3.cloned.1.call-done) | copy-start | bytes 5419012
  205.0 6.5 %copy-start.3 = (f32[96,672]{1,0:T(8,128)}, f32[96,672]{1,0:T(8,128)S(1)}, u32[]{:S(2)}) copy-start(f32[96,672]{1,0:T(8,128)S(1)} %fusion.22) | copy-start | bytes 774148
  367.7 22.1 %copy-start.2 = (f32[672,672]{1,0:T(8,128)S(1)}, f32[672,672]{1,0:T(8,128)}, u32[]{:S(2)}) copy-start(f32[672,672]{1,0:T(8,128)} %all-reduce.5.cloned.1.call-done) | copy-start | bytes 5419012
  410.5 10.5 %copy-start.4 = (f32[96,672]{1,0:T(8,128)}, f32[96,672]{1,0:T(8,128)S(1)}, u32[]{:S(2)}) copy-start(f32[96,672]{1,0:T(8,128)S(1)} %fusion.17) | copy-start | bytes 774148
Sparse Core Ops, SparseCore 0:
  25.5 136.9 all-reduce.2
  234.6 133.0 all-reduce.4
where the time goes:
time: 434 us; the launch traced here: 428 us
  waiting for transfers between devices  270 us (62%)
  other arithmetic  70.1 us (16%)
  matrix products  42.8 us (10%)
  blocking collectives  29 us (7%)
  between operations  14.8 us (3%)
    psum x1, waiting for transfers between devices, local(): gram_one = lax.psum(block_gram, ('grp', 'slab'))  137 us
    psum x1, waiting for transfers between devices, local(): gram_two = lax.psum(block_second, ('grp', 'slab'))  133 us
    another operation x12, other arithmetic, orthonormal(): lower_small = jnp.linalg.cholesky(cross)  38 us
    another operation x8, other arithmetic, orthonormal(): lax.linalg.triangular_solve(lower_small, widened, left_side=False, lower=...  32 us
    all_to_all x1, blocking collectives, local(): lax.all_to_all(reduced, 'grp', split_axis=1, concat_axis=0, tiled=True)  19.8 us
    dot_general x1, matrix products, local(): block_gram = jnp.einsum('jmi,jmk->ik', tensor, tensor, precision=HIGH)  18.1 us
    dot_general x4, matrix products, iterate_basis(): current = orthonormal(jnp.dot(gram, current, precision=HIGH))  11.3 us
    all_to_all x1, blocking collectives, local(): lax.all_to_all(core_block, 'grp', split_axis=0, concat_axis=1, tiled=True)  9.24 us
  transfers between devices with their start and end apart: 2, of which 2 were waited for; matrix products, arithmetic and copies ran while one was open for 0% of the time, Pallas kernels for 0%

commit v1 on v0

v1 whole, which is shorter than its diff:
```python
import functools

import jax
import jax.numpy as jnp
from jax import lax
from jax.experimental import pallas as pl
from jax.experimental.pallas import tpu as pltpu
from jax.sharding import PartitionSpec as P

HIGH = lax.Precision.HIGHEST
F32, BF16 = jnp.float32, jnp.bfloat16
LANES = 128
NN = (((1,), (0,)), ((), ()))
NT = (((1,), (1,)), ((), ()))
TN = (((0,), (0,)), ((), ()))
TT = (((0,), (1,)), ((), ()))


def dot(a, b, dims=NN, precision=None):
    return lax.dot_general(a, b, dims, precision=precision, preferred_element_type=F32)


def split(value):
    high = value.astype(BF16)
    low = (value - high.astype(F32)).astype(BF16)
    return high, low


def stacked(value, height):
    high, low = split(value)
    pad = jnp.zeros((height - value.shape[0], value.shape[1]), BF16)
    if pad.shape[0]:
        high, low = (jnp.concatenate([half, pad], axis=0) for half in (high, low))
    return jnp.concatenate([high, low], axis=0)


def ceil_to(value, unit):
    return -(-value // unit) * unit


def packed_rows(rank, wide, devices):
    dense = -(-rank * wide // LANES)
    return devices * ceil_to(-(-dense // devices), 8)


def pack(value, out):
    rank, wide = value.shape
    whole, rest = divmod(wide, LANES)
    for t in range(whole):
        out[t * rank : (t + 1) * rank, :] = value[:, t * LANES : (t + 1) * LANES]
    row = whole * rank
    if rest:
        groups = LANES // rest
        height = rank // groups
        tail = value[:, whole * LANES :]
        out[row : row + height, :] = jnp.concatenate(
            [tail[q * height : (q + 1) * height, :] for q in range(groups)], axis=1
        )
        row += height
    if row < out.shape[0]:
        out[row:, :] = jnp.zeros((out.shape[0] - row, LANES), F32)


def unpack(ref, rank, wide):
    whole, rest = divmod(wide, LANES)
    parts = [ref[t * rank : (t + 1) * rank, :] for t in range(whole)]
    if rest:
        groups = LANES // rest
        height = rank // groups
        tail = ref[whole * rank : whole * rank + height, :]
        parts.append(
            jnp.concatenate([tail[:, q * rest : (q + 1) * rest] for q in range(groups)], axis=0)
        )
    return jnp.concatenate(parts, axis=1)


def cost(flops, moved):
    return pl.CostEstimate(flops=int(flops), bytes_accessed=int(moved), transcendentals=0)


def params():
    return pltpu.CompilerParams(vmem_limit_bytes=32 * 1024 * 1024)


def call(kernel, outs, args, flops, scratch=(), name=None):
    return pl.pallas_call(
        kernel,
        out_shape=outs,
        in_specs=[pl.BlockSpec(memory_space=pltpu.VMEM)] * len(args),
        out_specs=jax.tree.map(lambda _: pl.BlockSpec(memory_space=pltpu.VMEM), outs),
        scratch_shapes=list(scratch),
        compiler_params=params(),
        cost_estimate=cost(flops, sum(a.size * 4 for a in args)),
        name=name,
    )(*args)


def chunk_of(rows):
    return max(c for c in range(16, 513, 16) if rows % c == 0)


def gram_kernel(rank, wide, steps, transposed, x_ref, v_ref, out_ref, vcat, acc):
    step = pl.program_id(0)
    height = vcat.shape[0] // 2

    @pl.when(step == 0)
    def _():
        value = v_ref[...].T if transposed else unpack(v_ref, rank, wide)
        vcat[...] = stacked(value, height)
        acc[...] = jnp.zeros_like(acc)

    xh, xl = split(x_ref[...])
    both = dot(vcat[...], xh, NT)
    z = both[:height] + both[height:] + dot(vcat[:height, :], xl, NT)
    zcat = stacked(z, height)
    both = dot(zcat, xh)
    acc[...] += both[:height] + both[height:] + dot(zcat[:height, :], xl)

    @pl.when(step == steps - 1)
    def _():
        pack(acc[:rank, :], out_ref)


def gram_apply(x, v, rank, rows_out, transposed):
    rows, wide = x.shape
    chunk = chunk_of(rows)
    steps = rows // chunk
    height = ceil_to(rank, LANES)
    return pl.pallas_call(
        functools.partial(gram_kernel, rank, wide, steps, transposed),
        grid=(steps,),
        out_shape=jax.ShapeDtypeStruct((rows_out, LANES), F32),
        in_specs=[
            pl.BlockSpec((chunk, wide), lambda i: (i, 0)),
            pl.BlockSpec(v.shape, lambda i: (0, 0)),
        ],
        out_specs=pl.BlockSpec((rows_out, LANES), lambda i: (0, 0)),
        scratch_shapes=[pltpu.VMEM((2 * height, wide), BF16), pltpu.VMEM((height, wide), F32)],
        compiler_params=params(),
        cost_estimate=cost(12 * rows * wide * rank, 4 * rows * wide),
        name="gram_apply",
    )(x, v)


def project_kernel(rank, wide, cols, groups, x_ref, q_ref, m_ref, w_ref, out_ref, vcat, u):
    step = pl.program_id(0)
    steps = pl.num_programs(0)
    height = vcat.shape[0] // 2
    chunk = x_ref.shape[0]

    @pl.when(step == 0)
    def _():
        w = dot(m_ref[...], unpack(q_ref, rank, wide), precision=HIGH)
        w_ref[...] = w
        vcat[...] = stacked(w, height)

    xh, xl = split(x_ref[...])
    both = dot(xh, vcat[...], NT)
    u[pl.ds(pl.multiple_of(step * chunk, chunk), chunk), :] = (
        both[:, :height] + both[:, height:] + dot(xl, vcat[:height, :], NT)
    )

    @pl.when(step == steps - 1)
    def _():
        depth = u.shape[0] // cols
        per = cols // groups
        for g in range(groups):
            pieces = [u[pl.ds(g * per + k, depth, stride=cols), :][:, :rank] for k in range(per)]
            pack_block(jnp.concatenate(pieces, axis=1), out_ref.at[g])


def block_rows(depth, wide):
    whole, rest = divmod(wide, LANES)
    return whole * depth + (ceil_to(-(-depth // (LANES // rest)), 8) if rest else 0)


def pack_block(value, out):
    depth, wide = value.shape
    whole, rest = divmod(wide, LANES)
    for t in range(whole):
        out[t * depth : (t + 1) * depth, :] = value[:, t * LANES : (t + 1) * LANES]
    if rest:
        fold = LANES // rest
        height = ceil_to(-(-depth // fold), 8)
        tail = value[:, whole * LANES :]
        parts = []
        for q in range(fold):
            part = tail[q * height : min((q + 1) * height, depth), :]
            if part.shape[0] < height:
                part = jnp.concatenate([part, jnp.zeros((height - part.shape[0], rest), F32)], axis=0)
            parts.append(part)
        out[whole * depth :, :] = jnp.concatenate(parts, axis=1)


def unpack_block(ref, depth, wide):
    whole, rest = divmod(wide, LANES)
    parts = [ref[t * depth : (t + 1) * depth, :] for t in range(whole)]
    if rest:
        fold = LANES // rest
        height = ceil_to(-(-depth // fold), 8)
        tail = ref[whole * depth :, :]
        folded = [
            tail[: min(height, depth - q * height), q * rest : (q + 1) * rest] for q in range(fold)
        ]
        parts.append(jnp.concatenate(folded, axis=0))
    return jnp.concatenate(parts, axis=1)


def project(x, q, m, rank, cols, groups):
    rows, wide = x.shape
    chunk = chunk_of(rows)
    height = ceil_to(rank, LANES)
    out_rows = block_rows(rows // cols, (cols // groups) * rank)
    return pl.pallas_call(
        functools.partial(project_kernel, rank, wide, cols, groups),
        grid=(rows // chunk,),
        out_shape=(
            jax.ShapeDtypeStruct((rank, wide), F32),
            jax.ShapeDtypeStruct((groups, out_rows, LANES), F32),
        ),
        in_specs=[
            pl.BlockSpec((chunk, wide), lambda i: (i, 0)),
            pl.BlockSpec(q.shape, lambda i: (0, 0)),
            pl.BlockSpec(m.shape, lambda i: (0, 0)),
        ],
        out_specs=(
            pl.BlockSpec((rank, wide), lambda i: (0, 0)),
            pl.BlockSpec((groups, out_rows, LANES), lambda i: (0, 0, 0)),
        ),
        scratch_shapes=[pltpu.VMEM((2 * height, wide), BF16), pltpu.VMEM((rows, height), F32)],
        compiler_params=params(),
        cost_estimate=cost(6 * rows * wide * rank, 4 * rows * wide),
        name="project",
    )(x, q, m)


def inverse_factor(cross, aug):
    rank = cross.shape[0]
    height, width = aug.shape[0], aug.shape[1] // 2
    row = lax.broadcasted_iota(jnp.int32, (height, width), 0)
    lane = lax.broadcasted_iota(jnp.int32, (height, width), 1)
    eye = (row == lane).astype(F32)
    aug[:, width:] = eye
    aug[:, :width] = eye
    aug[:rank, :rank] = cross
    sub = lax.broadcasted_iota(jnp.int32, (8, 1), 0)
    lane8 = lax.broadcasted_iota(jnp.int32, (8, width), 1)

    def panel(index, carry):
        first = pl.multiple_of(index * 8, 8)
        block = aug[pl.ds(first, 8), :]
        left = block[:, :width]
        columns = [
            jnp.sum(jnp.where(lane8 == first + c, left, 0.0), axis=1, keepdims=True) for c in range(8)
        ]
        pivots = jnp.ones((8, 1), F32)
        for r in range(8):
            pivot = columns[r][r : r + 1, :]
            factor = jnp.where(sub > r, columns[r] / pivot, 0.0)
            pivots = jnp.where(sub == r, pivot, pivots)
            block = block - factor * block[r : r + 1, :]
            for c in range(r + 1, 8):
                columns[c] = columns[c] - factor * columns[c][r : r + 1, :]
        block = block / jnp.sqrt(pivots)
        aug[pl.ds(first, 8), :] = block
        below = jnp.where(lane8 >= first + 8, block[:, :width], 0.0)
        aug[...] -= dot(below, block, TN, precision=HIGH)[:height]
        return carry

    lax.fori_loop(0, -(-rank // 8), panel, 0)
    return aug[:rank, width : width + rank]


def aug_scratch(rank):
    width = ceil_to(rank, LANES)
    return pltpu.VMEM((width, 2 * width), F32)


def factor_packed_kernel(rank, wide, w_ref, m_ref, aug):
    w = unpack(w_ref, rank, wide)
    m_ref[...] = inverse_factor(dot(w, w, NT, precision=HIGH), aug)


def factor_packed(w, rank, wide):
    return call(
        functools.partial(factor_packed_kernel, rank, wide),
        jax.ShapeDtypeStruct((rank, rank), F32),
        (w,),
        3e9,
        [aug_scratch(rank)],
        name="factor_packed",
    )


def factor_basis_kernel(rank, w_ref, m_ref, basis_ref, aug):
    w = w_ref[...]
    m = inverse_factor(dot(w, w, NT, precision=HIGH), aug)
    m_ref[...] = m
    basis_ref[...] = dot(w, m, TT, precision=HIGH)


def factor_basis(w):
    rank, wide = w.shape
    return call(
        functools.partial(factor_basis_kernel, rank),
        (jax.ShapeDtypeStruct((rank, rank), F32), jax.ShapeDtypeStruct((wide, rank), F32)),
        (w,),
        3e9,
        [aug_scratch(rank)],
        name="factor_basis",
    )


def second_kernel(rank, per, depth, u_ref, m_ref, start_ref, y_ref, out_ref):
    groups = u_ref.shape[0]
    for g in range(groups):
        block = unpack_block(u_ref.at[g], depth, per * rank)
        for k in range(per):
            y_ref[k, g * depth : (g + 1) * depth, :] = dot(
                block[:, k * rank : (k + 1) * rank], m_ref[...], NT, precision=HIGH
            )
    total = None
    for k in range(per):
        y = y_ref[k]
        term = dot(dot(start_ref[...], y, TN, precision=HIGH), y, NT, precision=HIGH)
        total = term if total is None else total + term
    pack(total, out_ref)


def second_first(u, m, start, per, rows_out):
    groups = u.shape[0]
    wide, rank2 = start.shape
    rank = m.shape[0]
    return call(
        functools.partial(second_kernel, rank, per, wide // groups),
        (
            jax.ShapeDtypeStruct((per, wide, rank), F32),
            jax.ShapeDtypeStruct((rows_out, LANES), F32),
        ),
        (u, m, start),
        1e8,
        name="second_first",
    )


def second_again_kernel(rank2, wide, y_ref, w_ref, out_ref):
    w = unpack(w_ref, rank2, wide)
    total = None
    for k in range(y_ref.shape[0]):
        y = y_ref[k]
        term = dot(dot(w, y, precision=HIGH), y, NT, precision=HIGH)
        total = term if total is None else total + term
    pack(total, out_ref)


def second_again(y, w, rank2, rows_out):
    return call(
        functools.partial(second_again_kernel, rank2, y.shape[1]),
        jax.ShapeDtypeStruct((rows_out, LANES), F32),
        (y, w),
        1e8,
        name="second_again",
    )


def last_kernel(rank2, wide, q_ref, m_ref, y_ref, basis_ref, core_ref, aug):
    w = dot(m_ref[...], unpack(q_ref, rank2, wide), precision=HIGH)
    m = inverse_factor(dot(w, w, NT, precision=HIGH), aug)
    basis_ref[...] = dot(w, m, TT, precision=HIGH)
    v = dot(m, w, precision=HIGH)
    for k in range(y_ref.shape[0]):
        block = dot(v, y_ref[k], precision=HIGH)
        height = core_ref.shape[2]
        for g in range(core_ref.shape[0]):
            core_ref[g, k] = block[g * height : (g + 1) * height, :]


def last(q, m, y, rank2, groups):
    per, wide, rank = y.shape
    return call(
        functools.partial(last_kernel, rank2, wide),
        (
            jax.ShapeDtypeStruct((wide, rank2), F32),
            jax.ShapeDtypeStruct((groups, per, rank2 // groups, rank), F32),
        ),
        (q, m, y),
        3e9,
        [aug_scratch(rank2)],
        name="last",
    )


def sum_kernel(in_ref, out_ref):
    total = in_ref[0]
    for d in range(1, in_ref.shape[0]):
        total = total + in_ref[d]
    for d in range(in_ref.shape[0]):
        out_ref[d] = total


def total_over(value, axes, devices):
    rows = value.shape[0]
    shares = lax.all_to_all(
        value.reshape(devices, rows // devices, LANES), axes, split_axis=0, concat_axis=0, tiled=True
    )
    copies = call(
        sum_kernel, jax.ShapeDtypeStruct(shares.shape, F32), (shares,), 1e6, name="share_sum"
    )
    whole = lax.all_to_all(copies, axes, split_axis=0, concat_axis=0, tiled=True)
    return whole.reshape(rows, LANES)


def local(groups, slabs, tensor, start_one, start_two):
    axes = ("grp", "slab")
    devices = groups * slabs
    depth, cols, wide = tensor.shape
    rank, rank2 = start_one.shape[1], start_two.shape[1]
    wide2 = start_two.shape[0]
    x = tensor.reshape(depth * cols, wide)
    rows = packed_rows(rank, wide, devices)
    rows2 = packed_rows(rank2, wide2, devices)
    per = cols // groups

    w1 = total_over(gram_apply(x, start_one, rank, rows, True), axes, devices)
    m1 = factor_packed(w1, rank, wide)
    q2 = total_over(gram_apply(x, w1, rank, rows, False), axes, devices)
    w2, u = project(x, q2, m1, rank, cols, groups)
    m2, basis_one = factor_basis(w2)
    u = lax.all_to_all(u, "grp", split_axis=0, concat_axis=0, tiled=True)
    y, p3 = second_first(u, m2, start_two, per, rows2)
    w3 = total_over(p3, axes, devices)
    m3 = factor_packed(w3, rank2, wide2)
    q4 = total_over(second_again(y, w3, rank2, rows2), axes, devices)
    basis_two, core = last(q4, m3, y, rank2, groups)
    core = lax.all_to_all(core, "grp", split_axis=0, concat_axis=0, tiled=True)
    core = core.transpose(2, 0, 1, 3).reshape(rank2 // groups, cols, rank)
    return (basis_one, basis_two, core)


def solution(mesh):
    groups, slabs = mesh.shape["grp"], mesh.shape["slab"]
    in_specs = (P("grp", "slab", None), P(), P())
    out_specs = (P(), P(), P("grp", "slab", None))
    return jax.shard_map(
        functools.partial(local, groups, slabs),
        mesh=mesh,
        in_specs=in_specs,
        out_specs=out_specs,
        check_vma=False,
    )
```

time: 434 us -> 168 us (0.39); the launches traced: 428 us -> 167 us
  waiting for transfers between devices: 270 us -> 20.6 us
  other arithmetic: 70.1 us -> 0 us
  blocking collectives: 29 us -> 81.4 us
  Pallas kernels: 0 us -> 44.4 us
  matrix products: 42.8 us -> 0 us
  between operations: 14.8 us -> 0.75 us
  starting transfers between devices: 0.25 us -> 12.1 us
  local copies, waits for them, and re-layouts: 1.15 us -> 8.04 us
    psum x2 -> x0, waiting for transfers between devices: 270 us -> none  [the longest x1 137 us: local(): gram_one = lax.psum(block_gram, ('grp', 'slab'))]
    another operation x20 -> x0, other arithmetic: 70.1 us -> none  [the longest x12 38 us: orthonormal(): lower_small = jnp.linalg.cholesky(cross)]
    all_to_all x2 -> x6, blocking collectives: 29 us -> 81.4 us  [the longest x4 55.9 us: total_over(): lax.all_to_all(value.reshape(devices, rows // devices, LANES), axes, spli...]
    pallas_call x0 -> x13, Pallas kernels: none -> 44.4 us  [the longest x10 34 us: call(): pl.pallas_call(kernel, out_shape=outs, in_specs=[pl.BlockSpec(memory_spac...]
    dot_general x12 -> x0, matrix products: 41 us -> none  [the longest x1 18.1 us: local(): block_gram = jnp.einsum('jmi,jmk->ik', tensor, tensor, precision=HIGH)]
    all_to_all x0 -> x4, waiting for transfers between devices: none -> 20.6 us  [the longest x2 8.59 us: total_over(): lax.all_to_all(copies, axes, split_axis=0, concat_axis=0, tiled=True)]
    all_to_all x0 -> x4, starting transfers between devices: none -> 12.1 us  [the longest x2 5.35 us: total_over(): lax.all_to_all(copies, axes, split_axis=0, concat_axis=0, tiled=True)]
    unnamed x10 -> x13, local copies, waits for them, and re-layouts: 0.03 us -> 8.04 us
  transfers between devices with their start and end apart: 2 -> 4, of which waited for: 2 -> 4; matrix products, arithmetic and copies ran while one was open for 0% -> 1% of each run, Pallas kernels for 0% -> 11%
where the time goes in v1:
time: 168 us; the launch traced here: 167 us
  blocking collectives  81.4 us (48%)
  Pallas kernels  44.4 us (26%)
  waiting for transfers between devices  20.6 us (12%)
  starting transfers between devices  12.1 us (7%)
  local copies, waits for them, and re-layouts  8.04 us (5%)
    all_to_all x4, blocking collectives, total_over(): lax.all_to_all(value.reshape(devices, rows // devices, LANES), axes, spli...  55.9 us
    pallas_call x10, Pallas kernels, call(): pl.pallas_call(kernel, out_shape=outs, in_specs=[pl.BlockSpec(memory_spac...  34 us
    all_to_all x2, blocking collectives, total_over(): lax.all_to_all(copies, axes, split_axis=0, concat_axis=0, tiled=True)  25.6 us
    all_to_all x2, waiting for transfers between devices, total_over(): lax.all_to_all(copies, axes, split_axis=0, concat_axis=0, tiled=True)  8.59 us
    unnamed x13, local copies, waits for them, and re-layouts  8.04 us
    all_to_all x1, waiting for transfers between devices, local(): u = lax.all_to_all(u, 'grp', split_axis=0, concat_axis=0, tiled=True)  7.98 us
    pallas_call x2, Pallas kernels, gram_apply(): pl.pallas_call(functools.partial(gram_kernel, rank, wide, steps, transpos...  7.29 us
    all_to_all x2, starting transfers between devices, total_over(): lax.all_to_all(copies, axes, split_axis=0, concat_axis=0, tiled=True)  5.35 us
  transfers between devices with their start and end apart: 4, of which 4 were waited for; matrix products, arithmetic and copies ran while one was open for 1% of the time, Pallas kernels for 11%

profile of v1, /device:TPU:0, one launch (start us, length us, event | category | flops | bytes accessed | tf_op | source)
XLA Modules:
  0.0 167.4 jit_solution(12080326760075490321)
XLA Ops:
  1.8 2.2 %copy-done = f32[168,8,672]{2,1,0:T(8,128)S(1)} copy-done((f32[168,8,672]{2,1,0:T(8,128)S(1)}, f32[168,8,672]{2,1,0:T(8,128)}, u32[]{:S(2)}) %copy-start) | copy-done | bytes 3612696
  3.9 3.7 %gram_apply.2 = f32[512,128]{1,0:T(8,128)S(1)} custom-call(f32[1344,672]{1,0:T(8,128)S(1)} %bitcast.12, f32[672,96]{1,0:T(8,128)S(1)} %copy.6.v_ref), custom_call_target="tpu_custom_call" | custom-call | flops 1040449536 | bytes 3612672 | tf_op jit(solution)/shard_map/gram_apply/pallas_call | solution.py:129
  7.6 17.7 %all_to_all.50.in_ref = f32[32,16,128]{2,1,0:T(8,128)S(1)} all-to-all(f32[32,16,128]{2,1,0:T(8,128)S(1)} %bitcast.20), channel_id=1, replica_groups=mesh['grp'=4,'slab'=8] {'grp','slab'}, dimensions={0} | all-to-all | bytes 524288 | tf_op jit(solution)/shard_map/all_to_all | solution.py:403
  25.4 12.8 %all_to_all.51 = f32[32,16,128]{2,1,0:T(8,128)S(1)} all-to-all(f32[32,16,128]{2,1,0:T(8,128)S(1)} %share_sum.4), channel_id=1, replica_groups=mesh['grp'=4,'slab'=8] {'grp','slab'}, dimensions={0} | all-to-all | bytes 524288 | tf_op jit(solution)/shard_map/all_to_all | solution.py:409
  38.2 3.6 %gram_apply.3 = f32[512,128]{1,0:T(8,128)S(1)} custom-call(f32[1344,672]{1,0:T(8,128)S(1)} %bitcast.13, f32[512,128]{1,0:T(8,128)S(1)} %bitcast.18), custom_call_target="tpu_custom_call" | custom-call | flops 1040449536 | bytes 3612672 | tf_op jit(solution)/shard_map/gram_apply/pallas_call | solution.py:129
  41.8 12.8 %all_to_all.52.in_ref = f32[32,16,128]{2,1,0:T(8,128)S(1)} all-to-all(f32[32,16,128]{2,1,0:T(8,128)S(1)} %bitcast.21), channel_id=1, replica_groups=mesh['grp'=4,'slab'=8] {'grp','slab'}, dimensions={0} | all-to-all | bytes 524288 | tf_op jit(solution)/shard_map/all_to_all | solution.py:403
  55.3 2.6 %all-to-all-start.3 = ((f32[32,16,128]{2,1,0:T(8,128)}), f32[32,16,128]{2,1,0:T(8,128)S(1)}, u32[]{:S(2)}, u32[]{:S(2)}) async-start(f32[32,16,128]{2,1,0:T(8,128)} %share_sum.5), calls=%async_computation.3 | async-start | bytes 524288 | tf_op jit(solution)/shard_map/all_to_all | solution.py:409
  57.9 6.2 %factor_packed.2.m_ref = f32[96,96]{1,0:T(8,128)S(1)} custom-call(f32[512,128]{1,0:T(8,128)S(1)} %bitcast.19), custom_call_target="tpu_custom_call" | custom-call | flops 3000000000 | bytes 262144 | tf_op jit(solution)/shard_map/factor_packed/pallas_call | solution.py:86
  64.1 4.4 %all-to-all-done.3 = f32[32,16,128]{2,1,0:T(8,128)S(1)} async-done(((f32[32,16,128]{2,1,0:T(8,128)}), f32[32,16,128]{2,1,0:T(8,128)S(1)}, u32[]{:S(2)}, u32[]{:S(2)}) %all-to-all-start.3) | async-done | bytes 262176 | tf_op jit(solution)/shard_map/all_to_all | solution.py:409
  68.5 2.2 %copy-done.2 = f32[168,8,672]{2,1,0:T(8,128)S(1)} copy-done((f32[168,8,672]{2,1,0:T(8,128)S(1)}, f32[168,8,672]{2,1,0:T(8,128)}, u32[]{:S(2)}) %copy-start.2) | copy-done | bytes 3612696
  70.6 3.1 %project.1 = (f32[96,672]{1,0:T(8,128)S(1)}, f32[4,256,128]{2,1,0:T(8,128)}) custom-call(f32[1344,672]{1,0:T(8,128)S(1)} %bitcast.14, f32[512,128]{1,0:T(8,128)S(1)} %bitcast.15, f32[96,96]{1,0:T(8,128)S(1)} %factor_packed.2.m_ref), custom_call_target="tpu_custom_call" | custom-call | flops 520224768 | bytes 3612672 | tf_op jit(solution)/shard_map/project/pallas_call | solution.py:214
  73.8 3.5 %all-to-all-start.4 = ((f32[4,256,128]{2,1,0:T(8,128)}), f32[4,256,128]{2,1,0:T(8,128)S(1)}, u32[]{:S(2)}, u32[]{:S(2)}) async-start(f32[4,256,128]{2,1,0:T(8,128)} %get-tuple-element.13), calls=%async_computation.4 | async-start | bytes 1048576 | tf_op jit(solution)/shard_map/all_to_all | solution.py:429
  77.4 6.7 %factor_basis.1 = (f32[96,96]{1,0:T(8,128)S(1)}, f32[672,96]{1,0:T(8,128)S(1)}) custom-call(f32[96,672]{1,0:T(8,128)S(1)} %get-tuple-element.11.w_ref), custom_call_target="tpu_custom_call" | custom-call | flops 3000000000 | bytes 258048 | tf_op jit(solution)/shard_map/factor_basis/pallas_call | solution.py:86
  84.1 8.0 %all-to-all-done.4.u_ref = f32[4,256,128]{2,1,0:T(8,128)S(1)} async-done(((f32[4,256,128]{2,1,0:T(8,128)}), f32[4,256,128]{2,1,0:T(8,128)S(1)}, u32[]{:S(2)}, u32[]{:S(2)}) %all-to-all-start.4) | async-done | bytes 524320 | tf_op jit(solution)/shard_map/all_to_all | solution.py:429
  92.1 3.2 %second_first.1 = (f32[2,672,96]{2,1,0:T(8,128)S(1)}, f32[512,128]{1,0:T(8,128)S(1)}) custom-call(f32[4,256,128]{2,1,0:T(8,128)S(1)} %all-to-all-done.4.u_ref, f32[96,96]{1,0:T(8,128)S(1)} %get-tuple-element.14.m_ref, f32[672,96]{1,0:T(8,128)S(1)} %copy.7.start_ref), custom_call_target="tpu_custom_call" | custom-call | flops 100000000 | bytes 819200 | tf_op jit(solution)/shard_map/second_first/pallas_call | solution.py:86
  95.2 12.6 %all_to_all.53.in_ref = f32[32,16,128]{2,1,0:T(8,128)S(1)} all-to-all(f32[32,16,128]{2,1,0:T(8,128)S(1)} %bitcast.24), channel_id=1, replica_groups=mesh['grp'=4,'slab'=8] {'grp','slab'}, dimensions={0} | all-to-all | bytes 524288 | tf_op jit(solution)/shard_map/all_to_all | solution.py:403
  107.9 12.8 %all_to_all.54 = f32[32,16,128]{2,1,0:T(8,128)S(1)} all-to-all(f32[32,16,128]{2,1,0:T(8,128)S(1)} %share_sum.6), channel_id=1, replica_groups=mesh['grp'=4,'slab'=8] {'grp','slab'}, dimensions={0} | all-to-all | bytes 524288 | tf_op jit(solution)/shard_map/all_to_all | solution.py:409
  122.4 12.8 %all_to_all.55.in_ref = f32[32,16,128]{2,1,0:T(8,128)S(1)} all-to-all(f32[32,16,128]{2,1,0:T(8,128)S(1)} %bitcast.22), channel_id=1, replica_groups=mesh['grp'=4,'slab'=8] {'grp','slab'}, dimensions={0} | all-to-all | bytes 524288 | tf_op jit(solution)/shard_map/all_to_all | solution.py:403
  135.9 2.8 %all-to-all-start.8 = ((f32[32,16,128]{2,1,0:T(8,128)}), f32[32,16,128]{2,1,0:T(8,128)S(1)}, u32[]{:S(2)}, u32[]{:S(2)}) async-start(f32[32,16,128]{2,1,0:T(8,128)} %share_sum.7), calls=%async_computation.8 | async-start | bytes 524288 | tf_op jit(solution)/shard_map/all_to_all | solution.py:409
  138.7 6.2 %factor_packed.3.m_ref = f32[96,96]{1,0:T(8,128)S(1)} custom-call(f32[512,128]{1,0:T(8,128)S(1)} %bitcast.17), custom_call_target="tpu_custom_call" | custom-call | flops 3000000000 | bytes 262144 | tf_op jit(solution)/shard_map/factor_packed/pallas_call | solution.py:86
  144.9 4.2 %all-to-all-done.8 = f32[32,16,128]{2,1,0:T(8,128)S(1)} async-done(((f32[32,16,128]{2,1,0:T(8,128)}), f32[32,16,128]{2,1,0:T(8,128)S(1)}, u32[]{:S(2)}, u32[]{:S(2)}) %all-to-all-start.8) | async-done | bytes 262176 | tf_op jit(solution)/shard_map/all_to_all | solution.py:409
  149.1 8.5 %last.1 = (f32[672,96]{1,0:T(8,128)S(1)}, f32[4,2,24,96]{3,2,1,0:T(8,128)}) custom-call(f32[512,128]{1,0:T(8,128)S(1)} %bitcast.23, f32[96,96]{1,0:T(8,128)S(1)} %factor_packed.3.m_ref, f32[2,672,96]{2,1,0:T(8,128)S(1)} %get-tuple-element.15.y_ref), custom_call_target="tpu_custom_call" | custom-call | flops 3000000000 | bytes 815104 | tf_op jit(solution)/shard_map/last/pallas_call | solution.py:86
  157.6 3.3 %all-to-all-start.9 = ((f32[4,2,24,96]{3,2,1,0:T(8,128)}), f32[4,2,24,96]{3,2,1,0:T(8,128)S(1)}, u32[]{:S(2)}, u32[]{:S(2)}) async-start(f32[4,2,24,96]{3,2,1,0:T(8,128)} %get-tuple-element.18), calls=%async_computation.9 | async-start | bytes 196608 | tf_op jit(solution)/shard_map/all_to_all | solution.py:435
  162.7 4.1 %all-to-all-done.9 = f32[4,2,24,96]{3,2,1,0:T(8,128)S(1)} async-done(((f32[4,2,24,96]{3,2,1,0:T(8,128)}), f32[4,2,24,96]{3,2,1,0:T(8,128)S(1)}, u32[]{:S(2)}, u32[]{:S(2)}) %all-to-all-start.9) | async-done | bytes 73760 | tf_op jit(solution)/shard_map/all_to_all | solution.py:435
  (16 shorter events, 7.0 us)
Async XLA Ops:
  1.8 2.2 %copy-start = (f32[168,8,672]{2,1,0:T(8,128)S(1)}, f32[168,8,672]{2,1,0:T(8,128)}, u32[]{:S(2)}) copy-start(f32[168,8,672]{2,1,0:T(8,128)} %param.3) | copy-start | bytes 10838020
  3.9 34.2 %copy-start.1 = (f32[168,8,672]{2,1,0:T(8,128)S(1)}, f32[168,8,672]{2,1,0:T(8,128)}, u32[]{:S(2)}) copy-start(f32[168,8,672]{2,1,0:T(8,128)} %param.3) | copy-start | bytes 10838020
  55.3 13.2 %all-to-all-start.3 = ((f32[32,16,128]{2,1,0:T(8,128)}), f32[32,16,128]{2,1,0:T(8,128)S(1)}, u32[]{:S(2)}, u32[]{:S(2)}) async-start(f32[32,16,128]{2,1,0:T(8,128)} %share_sum.5), calls=%async_computation.3 | async-start | bytes 524288 | tf_op jit(solution)/shard_map/all_to_all | solution.py:409
  57.9 19.3 %copy-start.3 = (f32[672,96]{0,1:T(8,128)S(1)}, f32[672,96]{0,1:T(8,128)}, u32[]{:S(2)}) copy-start(f32[672,96]{0,1:T(8,128)} %param.5) | copy-start | bytes 774148
  68.5 2.2 %copy-start.2 = (f32[168,8,672]{2,1,0:T(8,128)S(1)}, f32[168,8,672]{2,1,0:T(8,128)}, u32[]{:S(2)}) copy-start(f32[168,8,672]{2,1,0:T(8,128)} %param.3) | copy-start | bytes 10838020
  73.8 18.3 %all-to-all-start.4 = ((f32[4,256,128]{2,1,0:T(8,128)}), f32[4,256,128]{2,1,0:T(8,128)S(1)}, u32[]{:S(2)}, u32[]{:S(2)}) async-start(f32[4,256,128]{2,1,0:T(8,128)} %get-tuple-element.13), calls=%async_computation.4 | async-start | bytes 1048576 | tf_op jit(solution)/shard_map/all_to_all | solution.py:429
  135.9 13.2 %all-to-all-start.8 = ((f32[32,16,128]{2,1,0:T(8,128)}), f32[32,16,128]{2,1,0:T(8,128)S(1)}, u32[]{:S(2)}, u32[]{:S(2)}) async-start(f32[32,16,128]{2,1,0:T(8,128)} %share_sum.7), calls=%async_computation.8 | async-start | bytes 524288 | tf_op jit(solution)/shard_map/all_to_all | solution.py:409
  157.6 9.1 %all-to-all-start.9 = ((f32[4,2,24,96]{3,2,1,0:T(8,128)}), f32[4,2,24,96]{3,2,1,0:T(8,128)S(1)}, u32[]{:S(2)}, u32[]{:S(2)}) async-start(f32[4,2,24,96]{3,2,1,0:T(8,128)} %get-tuple-element.18), calls=%async_computation.9 | async-start | bytes 196608 | tf_op jit(solution)/shard_map/all_to_all | solution.py:435

commit v2 on v1

v2 whole, which is shorter than its diff:
```python
import functools

import jax
import jax.numpy as jnp
from jax import lax
from jax.experimental import pallas as pl
from jax.experimental.pallas import tpu as pltpu
from jax.sharding import PartitionSpec as P

HIGH = lax.Precision.HIGHEST
F32, BF16 = jnp.float32, jnp.bfloat16
LANES = 128
PANEL = 16
NN = (((1,), (0,)), ((), ()))
NT = (((1,), (1,)), ((), ()))
TN = (((0,), (0,)), ((), ()))


def dot(a, b, dims=NN, precision=None):
    return lax.dot_general(a, b, dims, precision=precision, preferred_element_type=F32)


def split(value):
    high = value.astype(BF16)
    low = (value - high.astype(F32)).astype(BF16)
    return high, low


def thirds(value):
    high = value.astype(BF16)
    rest = value - high.astype(F32)
    middle = rest.astype(BF16)
    return high, middle, (rest - middle.astype(F32)).astype(BF16)


def stacked(value, height):
    high, low = split(value)
    pad = jnp.zeros((height - value.shape[0], value.shape[1]), BF16)
    if pad.shape[0]:
        high, low = (jnp.concatenate([half, pad], axis=0) for half in (high, low))
    return jnp.concatenate([high, low], axis=0)


def ceil_to(value, unit):
    return -(-value // unit) * unit


def packed_rows(rank, wide, devices):
    dense = -(-rank * wide // LANES)
    return devices * ceil_to(-(-dense // devices), 8)


def pack(value, out):
    rank, wide = value.shape
    whole, rest = divmod(wide, LANES)
    for t in range(whole):
        out[t * rank : (t + 1) * rank, :] = value[:, t * LANES : (t + 1) * LANES]
    row = whole * rank
    if rest:
        groups = LANES // rest
        height = rank // groups
        tail = value[:, whole * LANES :]
        out[row : row + height, :] = jnp.concatenate(
            [tail[q * height : (q + 1) * height, :] for q in range(groups)], axis=1
        )
        row += height
    if row < out.shape[0]:
        out[row:, :] = jnp.zeros((out.shape[0] - row, LANES), F32)


def unpack(ref, rank, wide):
    whole, rest = divmod(wide, LANES)
    parts = [ref[t * rank : (t + 1) * rank, :] for t in range(whole)]
    if rest:
        groups = LANES // rest
        height = rank // groups
        tail = ref[whole * rank : whole * rank + height, :]
        parts.append(
            jnp.concatenate([tail[:, q * rest : (q + 1) * rest] for q in range(groups)], axis=0)
        )
    return jnp.concatenate(parts, axis=1)


def cost(flops, moved):
    return pl.CostEstimate(flops=int(flops), bytes_accessed=int(moved), transcendentals=0)


def in_hbm(array):
    return pltpu.with_memory_space_constraint(array, pltpu.HBM)


def in_vmem(array):
    return pltpu.with_memory_space_constraint(array, pltpu.VMEM)


def params():
    return pltpu.CompilerParams(vmem_limit_bytes=20 * 1024 * 1024)


def call(kernel, outs, args, flops, scratch=(), name=None, hbm=()):
    return pl.pallas_call(
        kernel,
        out_shape=outs,
        in_specs=[
            pl.BlockSpec(memory_space=pltpu.HBM if i in hbm else pltpu.VMEM) for i in range(len(args))
        ],
        out_specs=jax.tree.map(lambda _: pl.BlockSpec(memory_space=pltpu.VMEM), outs),
        scratch_shapes=list(scratch),
        compiler_params=params(),
        cost_estimate=cost(flops, sum(a.size * 4 for a in args)),
        name=name,
    )(*args)


def chunk_of(rows):
    return max(c for c in range(16, 513, 16) if rows % c == 0)


def gram_chunk(xh, xl, vcat):
    height = vcat.shape[0] // 2
    both = dot(vcat[...], xh, NT)
    z = both[:height] + both[height:] + dot(vcat[:height, :], xl, NT)
    zcat = stacked(z, height)
    both = dot(zcat, xh)
    return both[:height] + both[height:] + dot(zcat[:height, :], xl)


def low_reads(hbm, buffer, sems):
    steps, chunk, _ = buffer.shape
    return [
        pltpu.make_async_copy(hbm.at[pl.ds(i * chunk, chunk), :], buffer.at[i], sems.at[i])
        for i in range(steps)
    ]


def low_scratch(rows, wide):
    chunk = chunk_of(rows)
    return [
        pltpu.VMEM((rows // chunk, chunk, wide), BF16),
        pltpu.SemaphoreType.DMA((rows // chunk,)),
    ]


def gram_first_kernel(x_hbm, v_hbm, out_ref, xh_ref, xl_ref, xbuf, vbuf, vcat, sems):
    steps, chunk, _ = xbuf.shape
    start = pltpu.make_async_copy(v_hbm, vbuf, sems.at[steps])
    start.start()
    copies = [
        pltpu.make_async_copy(x_hbm.at[pl.ds(i * chunk, chunk), :], xbuf.at[i], sems.at[i])
        for i in range(steps)
    ]
    for copy in copies:
        copy.start()
    start.wait()
    vcat[...] = stacked(vbuf[...], vcat.shape[0] // 2)
    total = None
    for i in range(steps):
        copies[i].wait()
        xh, xl = split(xbuf[i])
        xh_ref[i * chunk : (i + 1) * chunk, :] = xh
        xl_ref[i * chunk : (i + 1) * chunk, :] = xl
        term = gram_chunk(xh, xl, vcat)
        total = term if total is None else total + term
    pack(total[: vbuf.shape[0], :], out_ref)


def gram_first(x, v, rows_out):
    rows, wide = x.shape
    rank = v.shape[0]
    chunk = chunk_of(rows)
    height = ceil_to(rank, LANES)
    vmem = pl.BlockSpec(memory_space=pltpu.VMEM)
    hbm = pl.BlockSpec(memory_space=pltpu.HBM)
    return pl.pallas_call(
        gram_first_kernel,
        out_shape=(
            jax.ShapeDtypeStruct((rows_out, LANES), F32),
            pltpu.VMEM((rows, wide), BF16),
            pltpu.VMEM((rows, wide), BF16),
        ),
        in_specs=[hbm, hbm],
        out_specs=(vmem, vmem, vmem),
        scratch_shapes=[
            pltpu.VMEM((rows // chunk, chunk, wide), F32),
            pltpu.VMEM((rank, wide), F32),
            pltpu.VMEM((2 * height, wide), BF16),
            pltpu.SemaphoreType.DMA((rows // chunk + 1,)),
        ],
        compiler_params=params(),
        cost_estimate=cost(12 * rows * wide * rank, 8 * rows * wide),
        name="gram_first",
    )(in_hbm(x), in_hbm(v))


def gram_again_kernel(rank, xh_ref, xl_ref, w_ref, out_ref, vcat):
    rows, wide = xh_ref.shape
    chunk = chunk_of(rows)
    vcat[...] = stacked(unpack(w_ref, rank, wide), vcat.shape[0] // 2)
    total = None
    for i in range(rows // chunk):
        part = slice(i * chunk, (i + 1) * chunk)
        term = gram_chunk(xh_ref[part, :], xl_ref[part, :], vcat)
        total = term if total is None else total + term
    pack(total[:rank, :], out_ref)


def gram_again(xh, xl, w, rank, rows_out):
    rows, wide = xh.shape
    return call(
        functools.partial(gram_again_kernel, rank),
        jax.ShapeDtypeStruct((rows_out, LANES), F32),
        (in_vmem(xh), in_vmem(xl), w),
        12 * rows * wide * rank,
        [pltpu.VMEM((2 * ceil_to(rank, LANES), wide), BF16)],
        name="gram_again",
    )


def project_kernel(rank, cols, xh_ref, xl_hbm, q_ref, m_ref, w_ref, out_ref, vcat, u, lbuf, sems):
    rows, wide = xh_ref.shape
    chunk = chunk_of(rows)
    height = vcat.shape[0] // 2
    reads = low_reads(xl_hbm, lbuf, sems)
    for read in reads:
        read.start()
    w = dot(m_ref[...], unpack(q_ref, rank, wide), precision=HIGH)
    w_ref[...] = w
    vcat[...] = stacked(w, height)
    for i in range(rows // chunk):
        part = slice(i * chunk, (i + 1) * chunk)
        both = dot(xh_ref[part, :], vcat[...], NT)
        u[part, :] = both[:, :height] + both[:, height:]
    for i in range(rows // chunk):
        reads[i].wait()
        u[i * chunk : (i + 1) * chunk, :] += dot(lbuf[i], vcat[:height, :], NT)
    depth = rows // cols
    groups = out_ref.shape[0]
    per = cols // groups
    for g in range(groups):
        pieces = [u[pl.ds(g * per + k, depth, stride=cols), :][:, :rank] for k in range(per)]
        pack_block(jnp.concatenate(pieces, axis=1), out_ref.at[g])


def block_rows(depth, wide):
    whole, rest = divmod(wide, LANES)
    return whole * depth + (ceil_to(-(-depth // (LANES // rest)), 8) if rest else 0)


def pack_block(value, out):
    depth, wide = value.shape
    whole, rest = divmod(wide, LANES)
    for t in range(whole):
        out[t * depth : (t + 1) * depth, :] = value[:, t * LANES : (t + 1) * LANES]
    if rest:
        fold = LANES // rest
        height = ceil_to(-(-depth // fold), 8)
        tail = value[:, whole * LANES :]
        parts = []
        for q in range(fold):
            part = tail[q * height : min((q + 1) * height, depth), :]
            if part.shape[0] < height:
                part = jnp.concatenate([part, jnp.zeros((height - part.shape[0], rest), F32)], axis=0)
            parts.append(part)
        out[whole * depth :, :] = jnp.concatenate(parts, axis=1)


def unpack_block(ref, depth, wide):
    whole, rest = divmod(wide, LANES)
    parts = [ref[t * depth : (t + 1) * depth, :] for t in range(whole)]
    if rest:
        fold = LANES // rest
        height = ceil_to(-(-depth // fold), 8)
        tail = ref[whole * depth :, :]
        folded = [
            tail[: min(height, depth - q * height), q * rest : (q + 1) * rest] for q in range(fold)
        ]
        parts.append(jnp.concatenate(folded, axis=0))
    return jnp.concatenate(parts, axis=1)


def project(xh, xl, q, m, rank, cols, groups):
    rows, wide = xh.shape
    height = ceil_to(rank, LANES)
    out_rows = block_rows(rows // cols, (cols // groups) * rank)
    return call(
        functools.partial(project_kernel, rank, cols),
        (
            jax.ShapeDtypeStruct((rank, wide), F32),
            jax.ShapeDtypeStruct((groups, out_rows, LANES), F32),
        ),
        (in_vmem(xh), in_hbm(xl), q, m),
        6 * rows * wide * rank,
        [pltpu.VMEM((2 * height, wide), BF16), pltpu.VMEM((rows, height), F32)]
        + low_scratch(rows, wide),
        name="project",
        hbm=(1,),
    )


def inverse_factor(cross, aug):
    rank = cross.shape[0]
    height, width = aug.shape[0], aug.shape[1] // 2
    row = lax.broadcasted_iota(jnp.int32, (height, width), 0)
    lane = lax.broadcasted_iota(jnp.int32, (height, width), 1)
    eye = (row == lane).astype(F32)
    aug[:, width:] = eye
    aug[:, :width] = eye
    aug[:rank, :rank] = cross
    sub = lax.broadcasted_iota(jnp.int32, (PANEL, 1), 0)
    lanes = lax.broadcasted_iota(jnp.int32, (PANEL, width), 1)

    def panel(index, carry):
        first = pl.multiple_of(index * PANEL, PANEL)
        block = aug[pl.ds(first, PANEL), :]
        left = block[:, :width]
        columns = [
            jnp.sum(jnp.where(lanes == first + c, left, 0.0), axis=1, keepdims=True)
            for c in range(PANEL)
        ]
        pivots = jnp.ones((PANEL, 1), F32)
        for r in range(PANEL):
            pivot = columns[r][r : r + 1, :]
            factor = jnp.where(sub > r, columns[r] * (1.0 / pivot), 0.0)
            pivots = jnp.where(sub == r, pivot, pivots)
            block = block - factor * block[r : r + 1, :]
            for c in range(r + 1, PANEL):
                columns[c] = columns[c] - factor * columns[c][r : r + 1, :]
        block = block / jnp.sqrt(pivots)
        aug[pl.ds(first, PANEL), :] = block
        below = jnp.where(lanes >= first + PANEL, block[:, :width], 0.0)
        aug[...] -= stacked_product(below, block)[:height]
        return carry

    lax.fori_loop(0, -(-rank // PANEL), panel, 0)
    return aug[:rank, width : width + rank]


def stacked_product(a, b):
    ah, am, al = thirds(a)
    bh, bm, bl = thirds(b)
    return dot(
        jnp.concatenate([ah, ah, am, ah, al, am], axis=0),
        jnp.concatenate([bh, bm, bh, bl, bh, bm], axis=0),
        TN,
    )


def aug_scratch(rank):
    width = ceil_to(rank, LANES)
    return pltpu.VMEM((width, 2 * width), F32)


def factor_packed_kernel(rank, wide, w_ref, m_ref, aug):
    w = unpack(w_ref, rank, wide)
    m_ref[...] = inverse_factor(dot(w, w, NT, precision=HIGH), aug)


def factor_packed(w, rank, wide):
    return call(
        functools.partial(factor_packed_kernel, rank, wide),
        jax.ShapeDtypeStruct((rank, rank), F32),
        (w,),
        3e9,
        [aug_scratch(rank)],
        name="factor_packed",
    )


def factor_basis_kernel(rank, w_ref, m_ref, basis_ref, aug):
    w = w_ref[...]
    m = inverse_factor(dot(w, w, NT, precision=HIGH), aug)
    m_ref[...] = m
    basis_ref[...] = dot(m, w, precision=HIGH)


def factor_basis(w):
    rank, wide = w.shape
    return call(
        functools.partial(factor_basis_kernel, rank),
        (jax.ShapeDtypeStruct((rank, rank), F32), jax.ShapeDtypeStruct((rank, wide), F32)),
        (w,),
        3e9,
        [aug_scratch(rank)],
        name="factor_basis",
    )


def second_product(v, yh, yl):
    height = ceil_to(v.shape[0], 16)
    vcat = stacked(v, height)
    both = dot(vcat, yh)
    z = both[:height] + both[height:] + dot(vcat[:height, :], yl)
    zcat = stacked(z, height)
    both = dot(zcat, yh, NT)
    total = both[:height] + both[height:] + dot(zcat[:height, :], yl, NT)
    return total[: v.shape[0]]


def second_first_kernel(per, depth, u_ref, m_ref, start_ref, yh_ref, yl_ref, out_ref):
    rank = m_ref.shape[0]
    lanes = yh_ref.shape[1] // per
    for g in range(u_ref.shape[0]):
        block = unpack_block(u_ref.at[g], depth, per * rank)
        part = slice(g * depth, (g + 1) * depth)
        for k in range(per):
            y = dot(block[:, k * rank : (k + 1) * rank], m_ref[...], NT, precision=HIGH)
            pad = jnp.zeros((depth, lanes - rank), F32)
            y = jnp.concatenate([y, pad], axis=1) if lanes > rank else y
            high = y.astype(BF16).astype(F32)
            yh_ref[part, k * lanes : (k + 1) * lanes] = high
            yl_ref[part, k * lanes : (k + 1) * lanes] = y - high
    pack(
        second_product(start_ref[...], yh_ref[...].astype(BF16), yl_ref[...].astype(BF16)), out_ref
    )


def second_first(u, m, start, per, rows_out):
    groups = u.shape[0]
    rank2, wide = start.shape
    lanes = ceil_to(m.shape[0], LANES)
    halves = jax.ShapeDtypeStruct((wide, per * lanes), F32)
    return call(
        functools.partial(second_first_kernel, per, wide // groups),
        (halves, halves, jax.ShapeDtypeStruct((rows_out, LANES), F32)),
        (u, m, start),
        1e8,
        name="second_first",
    )


def second_again_kernel(rank2, yh_ref, yl_ref, w_ref, out_ref):
    w = unpack(w_ref, rank2, yh_ref.shape[0])
    pack(second_product(w, yh_ref[...].astype(BF16), yl_ref[...].astype(BF16)), out_ref)


def second_again(yh, yl, w, rank2, rows_out):
    return call(
        functools.partial(second_again_kernel, rank2),
        jax.ShapeDtypeStruct((rows_out, LANES), F32),
        (yh, yl, w),
        1e8,
        name="second_again",
    )


def last_kernel(rank, rank2, q_ref, m_ref, yh_ref, yl_ref, basis_ref, core_ref, aug):
    wide = yh_ref.shape[0]
    w = dot(m_ref[...], unpack(q_ref, rank2, wide), precision=HIGH)
    m = inverse_factor(dot(w, w, NT, precision=HIGH), aug)
    v = dot(m, w, precision=HIGH)
    basis_ref[...] = v
    height = ceil_to(rank2, 16)
    vcat = stacked(v, height)
    yh, yl = yh_ref[...].astype(BF16), yl_ref[...].astype(BF16)
    both = dot(vcat, yh)
    block = both[:height] + both[height:] + dot(vcat[:height, :], yl)
    groups, per, share, _ = core_ref.shape
    lanes = yh.shape[1] // per
    for k in range(per):
        for g in range(groups):
            core_ref[g, k] = block[g * share : (g + 1) * share, k * lanes : k * lanes + rank]


def last(q, m, yh, yl, per, rank, rank2, groups):
    wide = yh.shape[0]
    return call(
        functools.partial(last_kernel, rank, rank2),
        (
            jax.ShapeDtypeStruct((rank2, wide), F32),
            jax.ShapeDtypeStruct((groups, per, rank2 // groups, rank), F32),
        ),
        (q, m, yh, yl),
        3e9,
        [aug_scratch(rank2)],
        name="last",
    )


def sum_kernel(in_ref, out_ref):
    total = in_ref[0]
    for d in range(1, in_ref.shape[0]):
        total = total + in_ref[d]
    for d in range(in_ref.shape[0]):
        out_ref[d] = total


def total_over(value, axes, devices):
    rows = value.shape[0]
    shares = lax.all_to_all(
        value.reshape(devices, rows // devices, LANES), axes, split_axis=0, concat_axis=0, tiled=True
    )
    copies = call(
        sum_kernel, jax.ShapeDtypeStruct(shares.shape, F32), (shares,), 1e6, name="share_sum"
    )
    whole = lax.all_to_all(copies, axes, split_axis=0, concat_axis=0, tiled=True)
    return whole.reshape(rows, LANES)


def local(groups, slabs, tensor, start_one, start_two):
    axes = ("grp", "slab")
    devices = groups * slabs
    depth, cols, wide = tensor.shape
    rank, rank2 = start_one.shape[1], start_two.shape[1]
    wide2 = start_two.shape[0]
    x = tensor.reshape(depth * cols, wide)
    rows = packed_rows(rank, wide, devices)
    rows2 = packed_rows(rank2, wide2, devices)
    per = cols // groups

    p1, xh, xl = gram_first(x, start_one.T, rows)
    w1 = total_over(p1, axes, devices)
    m1 = factor_packed(w1, rank, wide)
    q2 = total_over(gram_again(xh, xl, w1, rank, rows), axes, devices)
    w2, u = project(xh, xl, q2, m1, rank, cols, groups)
    m2, basis_one = factor_basis(w2)
    u = lax.all_to_all(u, "grp", split_axis=0, concat_axis=0, tiled=True)
    yh, yl, p3 = second_first(u, m2, start_two.T, per, rows2)
    w3 = total_over(p3, axes, devices)
    m3 = factor_packed(w3, rank2, wide2)
    q4 = total_over(second_again(yh, yl, w3, rank2, rows2), axes, devices)
    basis_two, core = last(q4, m3, yh, yl, per, rank, rank2, groups)
    core = lax.all_to_all(core, "grp", split_axis=0, concat_axis=0, tiled=True)
    core = core.transpose(2, 0, 1, 3).reshape(rank2 // groups, cols, rank)
    return (basis_one.T, basis_two.T, core)


def solution(mesh):
    groups, slabs = mesh.shape["grp"], mesh.shape["slab"]
    in_specs = (P("grp", "slab", None), P(), P())
    out_specs = (P(), P(), P("grp", "slab", None))
    return jax.shard_map(
        functools.partial(local, groups, slabs),
        mesh=mesh,
        in_specs=in_specs,
        out_specs=out_specs,
        check_vma=False,
    )
```

time: 168 us -> 157 us (0.935)
  Pallas kernels: 44.4 us -> 31.2 us
  blocking collectives: 81.4 us -> 89.7 us
  local copies, waits for them, and re-layouts: 8.04 us -> 0.67 us
  waiting for transfers between devices: 20.6 us -> 25.4 us
  starting transfers between devices: 12.1 us -> 8.65 us
    all_to_all x0 -> x1, blocking collectives: none -> 8.2 us  [local(): core = lax.all_to_all(core, 'grp', split_axis=0, concat_axis=0, tiled=True)]
    pallas_call x10 -> x12, Pallas kernels: 34 us -> 26.1 us  [call(): pl.pallas_call(kernel, out_shape=outs, in_specs=[pl.BlockSpec(memory_spac...]
    unnamed x13 -> x5, local copies, waits for them, and re-layouts: 8.04 us -> 0.67 us
    all_to_all x2, waiting for transfers between devices: 8.59 us -> 14.9 us  [total_over(): lax.all_to_all(copies, axes, split_axis=0, concat_axis=0, tiled=True)]
    pallas_call x3 -> x1, Pallas kernels: 10.4 us -> 5.1 us  [gram_first(): pl.pallas_call(gram_first_kernel, out_shape=(jax.ShapeDtypeStruct((rows_o...]
    all_to_all x1 -> x0, waiting for transfers between devices: 4.05 us -> none  [local(): core = lax.all_to_all(core, 'grp', split_axis=0, concat_axis=0, tiled=True)]
    all_to_all x1 -> x0, starting transfers between devices: 3.3 us -> none  [local(): core = lax.all_to_all(core, 'grp', split_axis=0, concat_axis=0, tiled=True)]
    all_to_all x1, waiting for transfers between devices: 7.98 us -> 10.6 us  [local(): u = lax.all_to_all(u, 'grp', split_axis=0, concat_axis=0, tiled=True)]
  transfers between devices with their start and end apart: 4 -> 3, of which waited for: 4 -> 3; matrix products, arithmetic and copies ran while one was open for 1% -> 0% of each run, Pallas kernels for 11% -> 7%
where the time goes in v2:
time: 157 us; the launch traced here: 156 us
  blocking collectives  89.7 us (57%)
  Pallas kernels  31.2 us (20%)
  waiting for transfers between devices  25.4 us (16%)
  starting transfers between devices  8.65 us (6%)
    all_to_all x4, blocking collectives, total_over(): lax.all_to_all(value.reshape(devices, rows // devices, LANES), axes, spli...  55.9 us
    pallas_call x12, Pallas kernels, call(): pl.pallas_call(kernel, out_shape=outs, in_specs=[pl.BlockSpec(memory_spac...  26.1 us
    all_to_all x2, blocking collectives, total_over(): lax.all_to_all(copies, axes, split_axis=0, concat_axis=0, tiled=True)  25.6 us
    all_to_all x2, waiting for transfers between devices, total_over(): lax.all_to_all(copies, axes, split_axis=0, concat_axis=0, tiled=True)  14.9 us
    all_to_all x1, waiting for transfers between devices, local(): u = lax.all_to_all(u, 'grp', split_axis=0, concat_axis=0, tiled=True)  10.6 us
    all_to_all x1, blocking collectives, local(): core = lax.all_to_all(core, 'grp', split_axis=0, concat_axis=0, tiled=True)  8.2 us
    all_to_all x2, starting transfers between devices, total_over(): lax.all_to_all(copies, axes, split_axis=0, concat_axis=0, tiled=True)  5.17 us
    pallas_call x1, Pallas kernels, gram_first(): pl.pallas_call(gram_first_kernel, out_shape=(jax.ShapeDtypeStruct((rows_o...  5.1 us
  transfers between devices with their start and end apart: 3, of which 3 were waited for; matrix products, arithmetic and copies ran while one was open for 0% of the time, Pallas kernels for 7%

profile of v2, /device:TPU:0, one launch (start us, length us, event | category | flops | bytes accessed | tf_op | source)
XLA Modules:
  0.0 156.4 jit_solution(16556256520147712409)
XLA Ops:
  0.6 5.1 %gram_first.1 = (f32[512,128]{1,0:T(8,128)S(1)}, bf16[1344,672]{1,0:T(8,128)(2,1)S(1)}, bf16[1344,672]{1,0:T(8,128)(2,1)S(1)}) custom-call(f32[1344,672]{1,0:T(8,128)} %bitcast.27, f32[96,672]{1,0:T(8,128)} %bitcast.29), custom_call_target="tpu_custom_call" | custom-call | flops 1040449536 | bytes 7225344 | tf_op jit(solution)/shard_map/gram_first/pallas_call | solution.py:174
  5.8 17.7 %all_to_all.50.in_ref = f32[32,16,128]{2,1,0:T(8,128)S(1)} all-to-all(f32[32,16,128]{2,1,0:T(8,128)S(1)} %bitcast.26), channel_id=1, replica_groups=mesh['grp'=4,'slab'=8] {'grp','slab'}, dimensions={0} | all-to-all | bytes 524288 | tf_op jit(solution)/shard_map/all_to_all | solution.py:489
  23.5 12.8 %all_to_all.51 = f32[32,16,128]{2,1,0:T(8,128)S(1)} all-to-all(f32[32,16,128]{2,1,0:T(8,128)S(1)} %share_sum.4), channel_id=1, replica_groups=mesh['grp'=4,'slab'=8] {'grp','slab'}, dimensions={0} | all-to-all | bytes 524288 | tf_op jit(solution)/shard_map/all_to_all | solution.py:495
  36.3 3.0 %gram_again.1 = f32[512,128]{1,0:T(8,128)S(1)} custom-call(bf16[1344,672]{1,0:T(8,128)(2,1)S(1)} %get-tuple-element.15.xh_ref, bf16[1344,672]{1,0:T(8,128)(2,1)S(1)} %get-tuple-element.16.xl_ref.xl_hbm, f32[512,128]{1,0:T(8,128)S(1)} %bitcast.17), custom_call_target="tpu_custom_call" | custom-call | flops 1040449536 | bytes 7487488 | tf_op jit(solution)/shard_map/gram_again/pallas_call | solution.py:101
  39.3 12.8 %all_to_all.52.in_ref = f32[32,16,128]{2,1,0:T(8,128)S(1)} all-to-all(f32[32,16,128]{2,1,0:T(8,128)S(1)} %bitcast.19), channel_id=1, replica_groups=mesh['grp'=4,'slab'=8] {'grp','slab'}, dimensions={0} | all-to-all | bytes 524288 | tf_op jit(solution)/shard_map/all_to_all | solution.py:489
  52.1 0.8 share_sum.5
  52.8 2.6 %all-to-all-start.3 = ((f32[32,16,128]{2,1,0:T(8,128)}), f32[32,16,128]{2,1,0:T(8,128)S(1)}, u32[]{:S(2)}, u32[]{:S(2)}) async-start(f32[32,16,128]{2,1,0:T(8,128)} %share_sum.5), calls=%async_computation.3 | async-start | bytes 524288 | tf_op jit(solution)/shard_map/all_to_all | solution.py:495
  55.4 3.1 %factor_packed.2.m_ref = f32[96,96]{1,0:T(8,128)S(1)} custom-call(f32[512,128]{1,0:T(8,128)S(1)} %bitcast.18), custom_call_target="tpu_custom_call" | custom-call | flops 3000000000 | bytes 262144 | tf_op jit(solution)/shard_map/factor_packed/pallas_call | solution.py:101
  58.6 7.4 %all-to-all-done.3 = f32[32,16,128]{2,1,0:T(8,128)S(1)} async-done(((f32[32,16,128]{2,1,0:T(8,128)}), f32[32,16,128]{2,1,0:T(8,128)S(1)}, u32[]{:S(2)}, u32[]{:S(2)}) %all-to-all-start.3) | async-done | bytes 262176 | tf_op jit(solution)/shard_map/all_to_all | solution.py:495
  66.0 3.4 %project.1 = (f32[96,672]{1,0:T(8,128)S(1)}, f32[4,256,128]{2,1,0:T(8,128)}) custom-call(bf16[1344,672]{1,0:T(8,128)(2,1)S(1)} %get-tuple-element.15.xh_ref, bf16[1344,672]{1,0:T(8,128)(2,1)} %copy-done, f32[512,128]{1,0:T(8,128)S(1)} %bitcast.16, f32[96,96]{1,0:T(8,128)S(1)} %factor_packed.2.m_ref), custom_call_target="tpu_custom_call" | custom-call | flops 520224768 | bytes 7524352 | tf_op jit(solution)/shard_map/project/pallas_call | solution.py:101
  69.4 3.5 %all-to-all-start.4 = ((f32[4,256,128]{2,1,0:T(8,128)}), f32[4,256,128]{2,1,0:T(8,128)S(1)}, u32[]{:S(2)}, u32[]{:S(2)}) async-start(f32[4,256,128]{2,1,0:T(8,128)} %get-tuple-element.20), calls=%async_computation.4 | async-start | bytes 1048576 | tf_op jit(solution)/shard_map/all_to_all | solution.py:516
  72.9 4.2 %factor_basis.1 = (f32[96,96]{1,0:T(8,128)S(1)}, f32[96,672]{1,0:T(8,128)}) custom-call(f32[96,672]{1,0:T(8,128)S(1)} %get-tuple-element.18.w_ref), custom_call_target="tpu_custom_call" | custom-call | flops 3000000000 | bytes 258048 | tf_op jit(solution)/shard_map/factor_basis/pallas_call | solution.py:101
  77.2 10.6 %all-to-all-done.4.u_ref = f32[4,256,128]{2,1,0:T(8,128)S(1)} async-done(((f32[4,256,128]{2,1,0:T(8,128)}), f32[4,256,128]{2,1,0:T(8,128)S(1)}, u32[]{:S(2)}, u32[]{:S(2)}) %all-to-all-start.4) | async-done | bytes 524320 | tf_op jit(solution)/shard_map/all_to_all | solution.py:516
  87.7 2.0 %second_first.1 = (f32[672,256]{1,0:T(8,128)S(1)}, f32[672,256]{1,0:T(8,128)S(1)}, f32[512,128]{1,0:T(8,128)S(1)}) custom-call(f32[4,256,128]{2,1,0:T(8,128)S(1)} %all-to-all-done.4.u_ref, f32[96,96]{1,0:T(8,128)S(1)} %get-tuple-element.21.m_ref, f32[96,672]{1,0:T(8,128)S(1)} %bitcast.23), custom_call_target="tpu_custom_call" | custom-call | flops 100000000 | bytes 819200 | tf_op jit(solution)/shard_map/second_first/pallas_call | solution.py:101
  89.7 12.7 %all_to_all.53.in_ref = f32[32,16,128]{2,1,0:T(8,128)S(1)} all-to-all(f32[32,16,128]{2,1,0:T(8,128)S(1)} %bitcast.25), channel_id=1, replica_groups=mesh['grp'=4,'slab'=8] {'grp','slab'}, dimensions={0} | all-to-all | bytes 524288 | tf_op jit(solution)/shard_map/all_to_all | solution.py:489
  102.5 12.8 %all_to_all.54 = f32[32,16,128]{2,1,0:T(8,128)S(1)} all-to-all(f32[32,16,128]{2,1,0:T(8,128)S(1)} %share_sum.6), channel_id=1, replica_groups=mesh['grp'=4,'slab'=8] {'grp','slab'}, dimensions={0} | all-to-all | bytes 524288 | tf_op jit(solution)/shard_map/all_to_all | solution.py:495
  115.2 0.8 second_again.1
  116.1 12.8 %all_to_all.55.in_ref = f32[32,16,128]{2,1,0:T(8,128)S(1)} all-to-all(f32[32,16,128]{2,1,0:T(8,128)S(1)} %bitcast.22), channel_id=1, replica_groups=mesh['grp'=4,'slab'=8] {'grp','slab'}, dimensions={0} | all-to-all | bytes 524288 | tf_op jit(solution)/shard_map/all_to_all | solution.py:489
  128.9 0.8 share_sum.7
  129.6 2.6 %all-to-all-start.8 = ((f32[32,16,128]{2,1,0:T(8,128)}), f32[32,16,128]{2,1,0:T(8,128)S(1)}, u32[]{:S(2)}, u32[]{:S(2)}) async-start(f32[32,16,128]{2,1,0:T(8,128)} %share_sum.7), calls=%async_computation.8 | async-start | bytes 524288 | tf_op jit(solution)/shard_map/all_to_all | solution.py:495
  132.2 3.1 %factor_packed.3.m_ref = f32[96,96]{1,0:T(8,128)S(1)} custom-call(f32[512,128]{1,0:T(8,128)S(1)} %bitcast.21), custom_call_target="tpu_custom_call" | custom-call | flops 3000000000 | bytes 262144 | tf_op jit(solution)/shard_map/factor_packed/pallas_call | solution.py:101
  135.4 7.4 %all-to-all-done.8 = f32[32,16,128]{2,1,0:T(8,128)S(1)} async-done(((f32[32,16,128]{2,1,0:T(8,128)}), f32[32,16,128]{2,1,0:T(8,128)S(1)}, u32[]{:S(2)}, u32[]{:S(2)}) %all-to-all-start.8) | async-done | bytes 262176 | tf_op jit(solution)/shard_map/all_to_all | solution.py:495
  142.8 4.7 %last.1 = (f32[96,672]{1,0:T(8,128)}, f32[4,2,24,96]{3,2,1,0:T(8,128)S(1)}) custom-call(f32[512,128]{1,0:T(8,128)S(1)} %bitcast.24, f32[96,96]{1,0:T(8,128)S(1)} %factor_packed.3.m_ref, f32[672,256]{1,0:T(8,128)S(1)} %get-tuple-element.22.yh_ref, f32[672,256]{1,0:T(8,128)S(1)} %get-tuple-element.23.yl_ref), custom_call_target="tpu_custom_call" | custom-call | flops 3000000000 | bytes 1675264 | tf_op jit(solution)/shard_map/last/pallas_call | solution.py:101
  147.5 8.2 %all_to_all.56 = f32[4,2,24,96]{3,2,1,0:T(8,128)S(1)} all-to-all(f32[4,2,24,96]{3,2,1,0:T(8,128)S(1)} %get-tuple-element.26), channel_id=1, replica_groups=mesh['grp'=4,'slab'=8] {'grp'}, dimensions={0} | all-to-all | bytes 147456 | tf_op jit(solution)/shard_map/all_to_all | solution.py:522
  (7 shorter events, 0.8 us)
Async XLA Ops:
  5.7 33.6 %copy-start = (bf16[1344,672]{1,0:T(8,128)(2,1)}, bf16[1344,672]{1,0:T(8,128)(2,1)S(1)}, u32[]{:S(2)}) copy-start(bf16[1344,672]{1,0:T(8,128)(2,1)S(1)} %get-tuple-element.16.xl_ref.xl_hbm) | copy-start | bytes 5419012
  52.8 13.2 %all-to-all-start.3 = ((f32[32,16,128]{2,1,0:T(8,128)}), f32[32,16,128]{2,1,0:T(8,128)S(1)}, u32[]{:S(2)}, u32[]{:S(2)}) async-start(f32[32,16,128]{2,1,0:T(8,128)} %share_sum.5), calls=%async_computation.3 | async-start | bytes 524288 | tf_op jit(solution)/shard_map/all_to_all | solution.py:495
  69.4 18.3 %all-to-all-start.4 = ((f32[4,256,128]{2,1,0:T(8,128)}), f32[4,256,128]{2,1,0:T(8,128)S(1)}, u32[]{:S(2)}, u32[]{:S(2)}) async-start(f32[4,256,128]{2,1,0:T(8,128)} %get-tuple-element.20), calls=%async_computation.4 | async-start | bytes 1048576 | tf_op jit(solution)/shard_map/all_to_all | solution.py:516
  72.9 14.8 %copy-start.1 = (f32[672,96]{0,1:T(8,128)S(1)}, f32[672,96]{0,1:T(8,128)}, u32[]{:S(2)}) copy-start(f32[672,96]{0,1:T(8,128)} %param.5) | copy-start | bytes 774148
  129.6 13.2 %all-to-all-start.8 = ((f32[32,16,128]{2,1,0:T(8,128)}), f32[32,16,128]{2,1,0:T(8,128)S(1)}, u32[]{:S(2)}, u32[]{:S(2)}) async-start(f32[32,16,128]{2,1,0:T(8,128)} %share_sum.7), calls=%async_computation.8 | async-start | bytes 524288 | tf_op jit(solution)/shard_map/all_to_all | solution.py:495

commit v3 on v2

--- a/solution.py
+++ b/solution.py
@@ -5,12 +5,14 @@
 from jax import lax
 from jax.experimental import pallas as pl
 from jax.experimental.pallas import tpu as pltpu
+from jax.sharding import Mesh
 from jax.sharding import PartitionSpec as P
 
 HIGH = lax.Precision.HIGHEST
 F32, BF16 = jnp.float32, jnp.bfloat16
 LANES = 128
 PANEL = 16
+CORES = 2
 NN = (((1,), (0,)), ((), ()))
 NT = (((1,), (1,)), ((), ()))
 TN = (((0,), (0,)), ((), ()))
@@ -97,12 +99,15 @@
     return pltpu.CompilerParams(vmem_limit_bytes=20 * 1024 * 1024)
 
 
-def call(kernel, outs, args, flops, scratch=(), name=None, hbm=()):
+def call(kernel, outs, args, flops, scratch=(), name=None, hbm=(), smem=()):
     return pl.pallas_call(
         kernel,
         out_shape=outs,
         in_specs=[
-            pl.BlockSpec(memory_space=pltpu.HBM if i in hbm else pltpu.VMEM) for i in range(len(args))
+            pl.BlockSpec(
+                memory_space=pltpu.HBM if i in hbm else pltpu.SMEM if i in smem else pltpu.VMEM
+            )
+            for i in range(len(args))
         ],
         out_specs=jax.tree.map(lambda _: pl.BlockSpec(memory_space=pltpu.VMEM), outs),
         scratch_shapes=list(scratch),
@@ -385,94 +390,148 @@
     )
 
 
-def second_product(v, yh, yl):
-    height = ceil_to(v.shape[0], 16)
-    vcat = stacked(v, height)
-    both = dot(vcat, yh)
-    z = both[:height] + both[height:] + dot(vcat[:height, :], yl)
-    zcat = stacked(z, height)
-    both = dot(zcat, yh, NT)
-    total = both[:height] + both[height:] + dot(zcat[:height, :], yl, NT)
-    return total[: v.shape[0]]
-
-
-def second_first_kernel(per, depth, u_ref, m_ref, start_ref, yh_ref, yl_ref, out_ref):
+def merge(whole, core_ref, own, other):
+    half = own.shape[0]
+    core = core_ref[0]
+    whole[pl.ds(pl.multiple_of(core * half, half), half), :] = own
+    whole[pl.ds(pl.multiple_of((1 - core) * half, half), half), :] = other
+
+
+def six_products(a, b, dims):
+    height = ceil_to(a.shape[0], 16)
+    pad = jnp.zeros((height - a.shape[0], a.shape[1]), BF16)
+    parts = thirds(a)
+    if pad.shape[0]:
+        parts = [jnp.concatenate([part, pad], axis=0) for part in parts]
+    three = jnp.concatenate(parts, axis=0)
+    first = dot(three, b[0], dims)
+    second = dot(three[: 2 * height], b[1], dims)
+    third = dot(three[:height], b[2], dims)
+    total = (third + first[2 * height :] + second[height:]) + (first[height : 2 * height] + second[:height])
+    return (total + first[:height])[: a.shape[0]]
+
+
+def second_product(v, y):
+    return six_products(six_products(v, y, NN), y, NT)
+
+
+def second_first_kernel(per, depth, core_ref, own_ref, other_ref, m_ref, start_ref, *rest):
+    *y_refs, out_ref, buf = rest
     rank = m_ref.shape[0]
-    lanes = yh_ref.shape[1] // per
-    for g in range(u_ref.shape[0]):
-        block = unpack_block(u_ref.at[g], depth, per * rank)
-        part = slice(g * depth, (g + 1) * depth)
-        for k in range(per):
-            y = dot(block[:, k * rank : (k + 1) * rank], m_ref[...], NT, precision=HIGH)
-            pad = jnp.zeros((depth, lanes - rank), F32)
-            y = jnp.concatenate([y, pad], axis=1) if lanes > rank else y
-            high = y.astype(BF16).astype(F32)
-            yh_ref[part, k * lanes : (k + 1) * lanes] = high
-            yl_ref[part, k * lanes : (k + 1) * lanes] = y - high
-    pack(
-        second_product(start_ref[...], yh_ref[...].astype(BF16), yl_ref[...].astype(BF16)), out_ref
-    )
-
-
-def second_first(u, m, start, per, rows_out):
-    groups = u.shape[0]
+    half = start_ref.shape[0] // CORES
+    lanes = buf.shape[1] // (CORES * per)
+    pad = jnp.zeros((depth, lanes - rank), F32)
+    for c, u_ref in enumerate((own_ref, other_ref)):
+        for g in range(u_ref.shape[0]):
+            block = unpack_block(u_ref.at[g], depth, per * rank)
+            for k in range(per):
+                u = block[:, k * rank : (k + 1) * rank]
+                u = jnp.concatenate([u, pad], axis=1) if lanes > rank else u
+                place = (c * per + k) * lanes
+                buf[g * depth : (g + 1) * depth, place : place + lanes] = u
+    m = m_ref[...]
+    if lanes > rank:
+        m = jnp.concatenate([m, jnp.zeros((rank, lanes - rank), F32)], axis=1)
+        m = jnp.concatenate([m, jnp.zeros((lanes - rank, lanes), F32)], axis=0)
+    mt = jnp.concatenate(thirds(m), axis=0)
+    uh, um, ul = thirds(buf[...])
+    for k in range(CORES * per):
+        part = slice(k * lanes, (k + 1) * lanes)
+        first = dot(uh[:, part], mt, NT)
+        second = dot(um[:, part], mt[: 2 * lanes, :], NT)
+        y = first[:, 2 * lanes :] + second[:, lanes:] + dot(ul[:, part], mt[:lanes, :], NT)
+        y = y + (first[:, lanes : 2 * lanes] + second[:, :lanes]) + first[:, :lanes]
+        for y_ref, third in zip(y_refs, thirds(y)):
+            y_ref[:, part] = third
+    start = start_ref[pl.ds(pl.multiple_of(core_ref[0] * half, half), half), :]
+    pack(second_product(start, [y_ref[...] for y_ref in y_refs]), out_ref)
+
+
+def second_first(core, own, other, m, start, per, rows_out):
+    groups = own.shape[0]
     rank2, wide = start.shape
-    lanes = ceil_to(m.shape[0], LANES)
-    halves = jax.ShapeDtypeStruct((wide, per * lanes), F32)
+    columns = CORES * per * ceil_to(m.shape[0], LANES)
+    part = jax.ShapeDtypeStruct((wide, columns), BF16)
+    *y, out = call(
+        functools.partial(second_first_kernel, per, wide // groups),
+        (part, part, part, jax.ShapeDtypeStruct((rows_out, LANES), F32)),
+        (core, own, other, m, start),
+        1e8,
+        [pltpu.VMEM((wide, columns), F32)],
+        name="second_first",
+        smem=(0,),
+    )
+    return y, out
+
+
+def second_again_kernel(half, yh_ref, ym_ref, yl_ref, w_ref, out_ref):
+    w = unpack(w_ref, half, yh_ref.shape[0])
+    pack(second_product(w, [yh_ref[...], ym_ref[...], yl_ref[...]]), out_ref)
+
+
+def second_again(y, w, half, rows_out):
     return call(
-        functools.partial(second_first_kernel, per, wide // groups),
-        (halves, halves, jax.ShapeDtypeStruct((rows_out, LANES), F32)),
-        (u, m, start),
-        1e8,
-        name="second_first",
-    )
-
-
-def second_again_kernel(rank2, yh_ref, yl_ref, w_ref, out_ref):
-    w = unpack(w_ref, rank2, yh_ref.shape[0])
-    pack(second_product(w, yh_ref[...].astype(BF16), yl_ref[...].astype(BF16)), out_ref)
-
-
-def second_again(yh, yl, w, rank2, rows_out):
-    return call(
-        functools.partial(second_again_kernel, rank2),
+        functools.partial(second_again_kernel, half),
         jax.ShapeDtypeStruct((rows_out, LANES), F32),
-        (yh, yl, w),
+        (*y, w),
         1e8,
         name="second_again",
     )
 
 
-def last_kernel(rank, rank2, q_ref, m_ref, yh_ref, yl_ref, basis_ref, core_ref, aug):
-    wide = yh_ref.shape[0]
-    w = dot(m_ref[...], unpack(q_ref, rank2, wide), precision=HIGH)
+def factor_halves_kernel(half, core_ref, own_ref, other_ref, m_ref, whole, aug):
+    wide = whole.shape[1]
+    merge(whole, core_ref, unpack(own_ref, half, wide), unpack(other_ref, half, wide))
+    w = whole[...]
+    m_ref[...] = inverse_factor(dot(w, w, NT, precision=HIGH), aug)
+
+
+def factor_halves(core, own, other, half, wide):
+    rank2 = CORES * half
+    return call(
+        functools.partial(factor_halves_kernel, half),
+        jax.ShapeDtypeStruct((rank2, rank2), F32),
+        (core, own, other),
+        3e9,
+        [pltpu.VMEM((rank2, wide), F32), aug_scratch(rank2)],
+        name="factor_halves",
+        smem=(0,),
+    )
+
+
+def last_kernel(rank, core_ref, own_ref, other_ref, m_ref, yh_ref, ym_ref, basis_ref, out_ref, whole, aug):
+    rank2, wide = whole.shape
+    half = rank2 // CORES
+    merge(whole, core_ref, unpack(own_ref, half, wide), unpack(other_ref, half, wide))
+    w = dot(m_ref[...], whole[...], precision=HIGH)
     m = inverse_factor(dot(w, w, NT, precision=HIGH), aug)
     v = dot(m, w, precision=HIGH)
     basis_ref[...] = v
     height = ceil_to(rank2, 16)
     vcat = stacked(v, height)
-    yh, yl = yh_ref[...].astype(BF16), yl_ref[...].astype(BF16)
-    both = dot(vcat, yh)
-    block = both[:height] + both[height:] + dot(vcat[:height, :], yl)
-    groups, per, share, _ = core_ref.shape
-    lanes = yh.shape[1] // per
+    groups, per, share, _ = out_ref.shape
+    lanes = yh_ref.shape[1] // (CORES * per)
+    both = dot(vcat, yh_ref[:, : per * lanes])
+    block = both[:height] + both[height:] + dot(vcat[:height, :], ym_ref[:, : per * lanes])
     for k in range(per):
         for g in range(groups):
-            core_ref[g, k] = block[g * share : (g + 1) * share, k * lanes : k * lanes + rank]
-
-
-def last(q, m, yh, yl, per, rank, rank2, groups):
-    wide = yh.shape[0]
+            out_ref[g, k] = block[g * share : (g + 1) * share, k * lanes : k * lanes + rank]
+
+
+def last(core, own, other, m, y, per, rank, groups):
+    rank2 = m.shape[0]
+    wide = y[0].shape[0]
     return call(
-        functools.partial(last_kernel, rank, rank2),
+        functools.partial(last_kernel, rank),
         (
             jax.ShapeDtypeStruct((rank2, wide), F32),
             jax.ShapeDtypeStruct((groups, per, rank2 // groups, rank), F32),
         ),
-        (q, m, yh, yl),
+        (core, own, other, m, y[0], y[1]),
         3e9,
-        [aug_scratch(rank2)],
+        [pltpu.VMEM((rank2, wide), F32), aug_scratch(rank2)],
         name="last",
+        smem=(0,),
     )
 
 
@@ -496,42 +555,50 @@
     return whole.reshape(rows, LANES)
 
 
-def local(groups, slabs, tensor, start_one, start_two):
-    axes = ("grp", "slab")
-    devices = groups * slabs
+def local(groups, chips, tensor, start_one, start_two):
+    every, alike = ("grp", "chip", "core"), ("grp", "chip")
+    devices, partners = groups * chips * CORES, groups * chips
     depth, cols, wide = tensor.shape
     rank, rank2 = start_one.shape[1], start_two.shape[1]
     wide2 = start_two.shape[0]
     x = tensor.reshape(depth * cols, wide)
+    half = rank2 // CORES
     rows = packed_rows(rank, wide, devices)
-    rows2 = packed_rows(rank2, wide2, devices)
+    rows2 = packed_rows(half, wide2, partners)
     per = cols // groups
+    core = lax.axis_index("core").reshape(1)
+
+    def swap(value):
+        return lax.ppermute(value, "core", [(i, CORES - 1 - i) for i in range(CORES)])
 
     p1, xh, xl = gram_first(x, start_one.T, rows)
-    w1 = total_over(p1, axes, devices)
+    w1 = total_over(p1, every, devices)
     m1 = factor_packed(w1, rank, wide)
-    q2 = total_over(gram_again(xh, xl, w1, rank, rows), axes, devices)
+    q2 = total_over(gram_again(xh, xl, w1, rank, rows), every, devices)
     w2, u = project(xh, xl, q2, m1, rank, cols, groups)
     m2, basis_one = factor_basis(w2)
     u = lax.all_to_all(u, "grp", split_axis=0, concat_axis=0, tiled=True)
-    yh, yl, p3 = second_first(u, m2, start_two.T, per, rows2)
-    w3 = total_over(p3, axes, devices)
-    m3 = factor_packed(w3, rank2, wide2)
-    q4 = total_over(second_again(yh, yl, w3, rank2, rows2), axes, devices)
-    basis_two, core = last(q4, m3, yh, yl, per, rank, rank2, groups)
-    core = lax.all_to_all(core, "grp", split_axis=0, concat_axis=0, tiled=True)
-    core = core.transpose(2, 0, 1, 3).reshape(rank2 // groups, cols, rank)
-    return (basis_one.T, basis_two.T, core)
+    u, m2 = lax.optimization_barrier((u, m2))
+    y, p3 = second_first(core, u, swap(u), m2, start_two.T, per, rows2)
+    w3 = total_over(p3, alike, partners)
+    p4, w3_other = lax.optimization_barrier((second_again(y, w3, half, rows2), swap(w3)))
+    m3 = factor_halves(core, w3, w3_other, half, wide2)
+    q4, m3 = lax.optimization_barrier((total_over(p4, alike, partners), m3))
+    basis_two, out = last(core, q4, swap(q4), m3, y, per, rank, groups)
+    out = lax.all_to_all(out, "grp", split_axis=0, concat_axis=0, tiled=True)
+    out = out.transpose(2, 0, 1, 3).reshape(rank2 // groups, cols, rank)
+    return (basis_one.T, basis_two.T, out)
 
 
 def solution(mesh):
     groups, slabs = mesh.shape["grp"], mesh.shape["slab"]
-    in_specs = (P("grp", "slab", None), P(), P())
-    out_specs = (P(), P(), P("grp", "slab", None))
+    chips = slabs // CORES
+    fine = Mesh(mesh.devices.reshape(groups, chips, CORES), ("grp", "chip", "core"))
+    split_spec = P("grp", ("chip", "core"), None)
     return jax.shard_map(
-        functools.partial(local, groups, slabs),
-        mesh=mesh,
-        in_specs=in_specs,
-        out_specs=out_specs,
+        functools.partial(local, groups, chips),
+        mesh=fine,
+        in_specs=(split_spec, P(), P()),
+        out_specs=(P(), P(), split_spec),
         check_vma=False,
     )

time: 157 us -> 154 us (0.981)
  blocking collectives: 89.7 us -> 84.3 us
    all_to_all x4, blocking collectives: 55.9 us -> 52.4 us  [total_over(): lax.all_to_all(value.reshape(devices, rows // devices, LANES), axes, spli...]
    ppermute x0 -> x3, waiting for transfers between devices: none -> 3.4 us  [swap(): lax.ppermute(value, 'core', [(i, CORES - 1 - i) for i in range(CORES)])]
    all_to_all x2, waiting for transfers between devices: 14.9 us -> 12 us  [total_over(): lax.all_to_all(copies, axes, split_axis=0, concat_axis=0, tiled=True)]
    all_to_all x2, blocking collectives: 25.6 us -> 23.5 us  [total_over(): lax.all_to_all(copies, axes, split_axis=0, concat_axis=0, tiled=True)]
  transfers between devices with their start and end apart: 3 -> 6, of which waited for: 3 -> 6; matrix products, arithmetic and copies ran while one was open for 0% -> 0% of each run, Pallas kernels for 7% -> 8%
where the time goes in v3:
time: 154 us; the launch traced here: 153 us
  blocking collectives  84.3 us (55%)
  Pallas kernels  32.2 us (21%)
  waiting for transfers between devices  25.9 us (17%)
  starting transfers between devices  9.59 us (6%)
    all_to_all x4, blocking collectives, total_over(): lax.all_to_all(value.reshape(devices, rows // devices, LANES), axes, spli...  52.4 us
    pallas_call x12, Pallas kernels, call(): pl.pallas_call(kernel, out_shape=outs, in_specs=[pl.BlockSpec(memory_spac...  27.1 us
    all_to_all x2, blocking collectives, total_over(): lax.all_to_all(copies, axes, split_axis=0, concat_axis=0, tiled=True)  23.5 us
    all_to_all x2, waiting for transfers between devices, total_over(): lax.all_to_all(copies, axes, split_axis=0, concat_axis=0, tiled=True)  12 us
    all_to_all x1, waiting for transfers between devices, local(): u = lax.all_to_all(u, 'grp', split_axis=0, concat_axis=0, tiled=True)  10.6 us
    all_to_all x1, blocking collectives, local(): out = lax.all_to_all(out, 'grp', split_axis=0, concat_axis=0, tiled=True)  8.35 us
    all_to_all x2, starting transfers between devices, total_over(): lax.all_to_all(copies, axes, split_axis=0, concat_axis=0, tiled=True)  6.1 us
    pallas_call x1, Pallas kernels, gram_first(): pl.pallas_call(gram_first_kernel, out_shape=(jax.ShapeDtypeStruct((rows_o...  5.1 us
  transfers between devices with their start and end apart: 6, of which 6 were waited for; matrix products, arithmetic and copies ran while one was open for 0% of the time, Pallas kernels for 8%

profile of v3, /device:TPU:0, one launch (start us, length us, event | category | flops | bytes accessed | tf_op | source)
XLA Modules:
  0.0 153.4 jit_solution(99236187337715575)
XLA Ops:
  0.6 5.1 %gram_first.1 = (f32[512,128]{1,0:T(8,128)S(1)}, bf16[1344,672]{1,0:T(8,128)(2,1)S(1)}, bf16[1344,672]{1,0:T(8,128)(2,1)S(1)}) custom-call(f32[1344,672]{1,0:T(8,128)} %bitcast.30, f32[96,672]{1,0:T(8,128)} %bitcast.32), custom_call_target="tpu_custom_call" | custom-call | flops 1040449536 | bytes 7225344 | tf_op jit(solution)/shard_map/gram_first/pallas_call | solution.py:179
  5.7 17.7 %all_to_all.50.in_ref = f32[32,16,128]{2,1,0:T(8,128)S(1)} all-to-all(f32[32,16,128]{2,1,0:T(8,128)S(1)} %bitcast.26), channel_id=1, replica_groups=mesh['grp'=4,'chip'=4,'core'=2] {'grp','chip','core'}, dimensions={0} | all-to-all | bytes 524288 | tf_op jit(solution)/shard_map/all_to_all | solution.py:548
  23.5 12.8 %all_to_all.51 = f32[32,16,128]{2,1,0:T(8,128)S(1)} all-to-all(f32[32,16,128]{2,1,0:T(8,128)S(1)} %share_sum.4), channel_id=1, replica_groups=mesh['grp'=4,'chip'=4,'core'=2] {'grp','chip','core'}, dimensions={0} | all-to-all | bytes 524288 | tf_op jit(solution)/shard_map/all_to_all | solution.py:554
  36.3 3.0 %gram_again.1 = f32[512,128]{1,0:T(8,128)S(1)} custom-call(bf16[1344,672]{1,0:T(8,128)(2,1)S(1)} %get-tuple-element.22.xh_ref, bf16[1344,672]{1,0:T(8,128)(2,1)S(1)} %get-tuple-element.23.xl_ref.xl_hbm, f32[512,128]{1,0:T(8,128)S(1)} %bitcast.18), custom_call_target="tpu_custom_call" | custom-call | flops 1040449536 | bytes 7487488 | tf_op jit(solution)/shard_map/gram_again/pallas_call | solution.py:103
  39.3 12.8 %all_to_all.52.in_ref = f32[32,16,128]{2,1,0:T(8,128)S(1)} all-to-all(f32[32,16,128]{2,1,0:T(8,128)S(1)} %bitcast.20), channel_id=1, replica_groups=mesh['grp'=4,'chip'=4,'core'=2] {'grp','chip','core'}, dimensions={0} | all-to-all | bytes 524288 | tf_op jit(solution)/shard_map/all_to_all | solution.py:548
  52.8 2.6 %all-to-all-start.3 = ((f32[32,16,128]{2,1,0:T(8,128)}), f32[32,16,128]{2,1,0:T(8,128)S(1)}, u32[]{:S(2)}, u32[]{:S(2)}) async-start(f32[32,16,128]{2,1,0:T(8,128)} %share_sum.5), calls=%async_computation.3 | async-start | bytes 524288 | tf_op jit(solution)/shard_map/all_to_all | solution.py:554
  55.4 3.1 %factor_packed.1.m_ref = f32[96,96]{1,0:T(8,128)S(1)} custom-call(f32[512,128]{1,0:T(8,128)S(1)} %bitcast.19), custom_call_target="tpu_custom_call" | custom-call | flops 3000000000 | bytes 262144 | tf_op jit(solution)/shard_map/factor_packed/pallas_call | solution.py:103
  58.6 7.4 %all-to-all-done.3 = f32[32,16,128]{2,1,0:T(8,128)S(1)} async-done(((f32[32,16,128]{2,1,0:T(8,128)}), f32[32,16,128]{2,1,0:T(8,128)S(1)}, u32[]{:S(2)}, u32[]{:S(2)}) %all-to-all-start.3) | async-done | bytes 262176 | tf_op jit(solution)/shard_map/all_to_all | solution.py:554
  66.0 3.4 %project.1 = (f32[96,672]{1,0:T(8,128)S(1)}, f32[4,256,128]{2,1,0:T(8,128)}) custom-call(bf16[1344,672]{1,0:T(8,128)(2,1)S(1)} %get-tuple-element.22.xh_ref, bf16[1344,672]{1,0:T(8,128)(2,1)} %copy-done, f32[512,128]{1,0:T(8,128)S(1)} %bitcast.17, f32[96,96]{1,0:T(8,128)S(1)} %factor_packed.1.m_ref), custom_call_target="tpu_custom_call" | custom-call | flops 520224768 | bytes 7524352 | tf_op jit(solution)/shard_map/project/pallas_call | solution.py:103
  69.4 3.5 %all-to-all-start.4 = ((f32[4,256,128]{2,1,0:T(8,128)}), f32[4,256,128]{2,1,0:T(8,128)S(1)}, u32[]{:S(2)}, u32[]{:S(2)}) async-start(f32[4,256,128]{2,1,0:T(8,128)} %get-tuple-element.27), calls=%async_computation.4 | async-start | bytes 1048576 | tf_op jit(solution)/shard_map/all_to_all | solution.py:580
  72.9 4.2 %factor_basis.1 = (f32[96,96]{1,0:T(8,128)S(1)}, f32[96,672]{1,0:T(8,128)}) custom-call(f32[96,672]{1,0:T(8,128)S(1)} %get-tuple-element.25.w_ref), custom_call_target="tpu_custom_call" | custom-call | flops 3000000000 | bytes 258048 | tf_op jit(solution)/shard_map/factor_basis/pallas_call | solution.py:103
  77.2 10.6 %all-to-all-done.4.own_ref = f32[4,256,128]{2,1,0:T(8,128)S(1)} async-done(((f32[4,256,128]{2,1,0:T(8,128)}), f32[4,256,128]{2,1,0:T(8,128)S(1)}, u32[]{:S(2)}, u32[]{:S(2)}) %all-to-all-start.4) | async-done | bytes 524320 | tf_op jit(solution)/shard_map/all_to_all | solution.py:580
  87.7 1.9 %collective-permute-done.other_ref = f32[4,256,128]{2,1,0:T(8,128)S(1)} collective-permute-done((f32[4,256,128]{2,1,0:T(8,128)S(1)}, f32[4,256,128]{2,1,0:T(8,128)S(1)}, u32[]{:S(2)}, u32[]{:S(2)}) %collective-permute-start) | collective-permute-done | bytes 524320 | tf_op jit(solution)/shard_map/ppermute | solution.py:572
  89.6 2.6 %second_first.1 = (bf16[672,512]{1,0:T(8,128)(2,1)S(1)}, bf16[672,512]{1,0:T(8,128)(2,1)S(1)}, bf16[672,512]{1,0:T(8,128)(2,1)S(1)}, f32[256,128]{1,0:T(8,128)S(1)}) custom-call(s32[1]{0:T(128)} %bitcast.7.core_ref, f32[4,256,128]{2,1,0:T(8,128)S(1)} %all-to-all-done.4.own_ref, f32[4,256,128]{2,1,0:T(8,128)S(1)} %collective-permute-done.other_ref, ...), custom_call_target="tpu_custom_call" | custom-call | flops 100000000 | bytes 1343492 | tf_op jit(solution)/shard_map/second_first/pallas_call | solution.py:103
  92.2 10.9 %all_to_all.53.in_ref = f32[16,16,128]{2,1,0:T(8,128)S(1)} all-to-all(f32[16,16,128]{2,1,0:T(8,128)S(1)} %bitcast.29), channel_id=1, replica_groups=mesh['grp'=4,'chip'=4,'core'=2] {'grp','chip'}, dimensions={0} | all-to-all | bytes 262144 | tf_op jit(solution)/shard_map/all_to_all | solution.py:548
  103.2 10.7 %all_to_all.54 = f32[16,16,128]{2,1,0:T(8,128)S(1)} all-to-all(f32[16,16,128]{2,1,0:T(8,128)S(1)} %share_sum.6), channel_id=1, replica_groups=mesh['grp'=4,'chip'=4,'core'=2] {'grp','chip'}, dimensions={0} | all-to-all | bytes 262144 | tf_op jit(solution)/shard_map/all_to_all | solution.py:554
  113.9 1.2 second_again.1
  115.2 11.0 %all_to_all.55.in_ref = f32[16,16,128]{2,1,0:T(8,128)S(1)} all-to-all(f32[16,16,128]{2,1,0:T(8,128)S(1)} %bitcast.24), channel_id=1, replica_groups=mesh['grp'=4,'chip'=4,'core'=2] {'grp','chip'}, dimensions={0} | all-to-all | bytes 262144 | tf_op jit(solution)/shard_map/all_to_all | solution.py:548
  126.9 3.5 %all-to-all-start.8 = ((f32[16,16,128]{2,1,0:T(8,128)}), f32[16,16,128]{2,1,0:T(8,128)S(1)}, u32[]{:S(2)}, u32[]{:S(2)}) async-start(f32[16,16,128]{2,1,0:T(8,128)} %share_sum.7), calls=%async_computation.8 | async-start | bytes 262144 | tf_op jit(solution)/shard_map/all_to_all | solution.py:554
  130.4 3.2 %factor_halves.1.m_ref = f32[96,96]{1,0:T(8,128)S(1)} custom-call(s32[1]{0:T(128)} %bitcast.7.core_ref, f32[256,128]{1,0:T(8,128)S(1)} %bitcast.23, f32[256,128]{1,0:T(8,128)S(1)} %collective-permute-done.1.other_ref), custom_call_target="tpu_custom_call" | custom-call | flops 3000000000 | bytes 262148 | tf_op jit(solution)/shard_map/factor_halves/pallas_call | solution.py:103
  133.6 4.5 %all-to-all-done.8 = f32[16,16,128]{2,1,0:T(8,128)S(1)} async-done(((f32[16,16,128]{2,1,0:T(8,128)}), f32[16,16,128]{2,1,0:T(8,128)S(1)}, u32[]{:S(2)}, u32[]{:S(2)}) %all-to-all-start.8) | async-done | bytes 131104 | tf_op jit(solution)/shard_map/all_to_all | solution.py:554
  138.2 1.3 collective-permute-done.2.other_ref
  139.5 4.9 %last.1 = (f32[96,672]{1,0:T(8,128)}, f32[4,2,24,96]{3,2,1,0:T(8,128)S(1)}) custom-call(s32[1]{0:T(128)} %bitcast.7.core_ref, f32[256,128]{1,0:T(8,128)S(1)} %bitcast.28, f32[256,128]{1,0:T(8,128)S(1)} %collective-permute-done.2.other_ref, f32[96,96]{1,0:T(8,128)S(1)} %factor_halves.1.m_ref, bf16[672,512]{1,0:T(8,128)(2,1)S(1)} %get-tuple-element.31.yh_ref, ...), custom_call_target="tpu_custom_call" | custom-call | flops 3000000000 | bytes 3051524 | tf_op jit(solution)/shard_map/last/pallas_call | solution.py:103
  144.4 8.3 %all_to_all.56 = f32[4,2,24,96]{3,2,1,0:T(8,128)S(1)} all-to-all(f32[4,2,24,96]{3,2,1,0:T(8,128)S(1)} %get-tuple-element.40), channel_id=1, replica_groups=mesh['grp'=4,'chip'=4,'core'=2] {'grp'}, dimensions={0} | all-to-all | bytes 147456 | tf_op jit(solution)/shard_map/all_to_all | solution.py:588
  (13 shorter events, 2.3 us)
Async XLA Ops:
  5.7 33.6 %copy-start = (bf16[1344,672]{1,0:T(8,128)(2,1)}, bf16[1344,672]{1,0:T(8,128)(2,1)S(1)}, u32[]{:S(2)}) copy-start(bf16[1344,672]{1,0:T(8,128)(2,1)S(1)} %get-tuple-element.23.xl_ref.xl_hbm) | copy-start | bytes 5419012
  52.8 13.2 %all-to-all-start.3 = ((f32[32,16,128]{2,1,0:T(8,128)}), f32[32,16,128]{2,1,0:T(8,128)S(1)}, u32[]{:S(2)}, u32[]{:S(2)}) async-start(f32[32,16,128]{2,1,0:T(8,128)} %share_sum.5), calls=%async_computation.3 | async-start | bytes 524288 | tf_op jit(solution)/shard_map/all_to_all | solution.py:554
  69.4 18.3 %all-to-all-start.4 = ((f32[4,256,128]{2,1,0:T(8,128)}), f32[4,256,128]{2,1,0:T(8,128)S(1)}, u32[]{:S(2)}, u32[]{:S(2)}) async-start(f32[4,256,128]{2,1,0:T(8,128)} %get-tuple-element.27), calls=%async_computation.4 | async-start | bytes 1048576 | tf_op jit(solution)/shard_map/all_to_all | solution.py:580
  72.9 16.7 %copy-start.1 = (f32[672,96]{0,1:T(8,128)S(1)}, f32[672,96]{0,1:T(8,128)}, u32[]{:S(2)}) copy-start(f32[672,96]{0,1:T(8,128)} %param.5) | copy-start | bytes 774148
  87.7 1.9 %collective-permute-start = (f32[4,256,128]{2,1,0:T(8,128)S(1)}, f32[4,256,128]{2,1,0:T(8,128)S(1)}, u32[]{:S(2)}, u32[]{:S(2)}) collective-permute-start(f32[4,256,128]{2,1,0:T(8,128)S(1)} %all-to-all-done.4.own_ref), channel_id=1, source_target_pairs={{0,1},{1,0},{2,3},{3,2},{4,5},{5,4},{6,7},{7,6},{8,9},{9,8},{10,11... | collective-permute-start | bytes 1572872 | tf_op jit(solution)/shard_map/ppermute | solution.py:572
  113.9 1.3 collective-permute-start.1
  126.9 11.3 %all-to-all-start.8 = ((f32[16,16,128]{2,1,0:T(8,128)}), f32[16,16,128]{2,1,0:T(8,128)S(1)}, u32[]{:S(2)}, u32[]{:S(2)}) async-start(f32[16,16,128]{2,1,0:T(8,128)} %share_sum.7), calls=%async_computation.8 | async-start | bytes 262144 | tf_op jit(solution)/shard_map/all_to_all | solution.py:554
  138.2 1.3 collective-permute-start.2
